TPU v7x, 8 devices: a whole 2x2x1 slice. The times are simulated.
8 devices in a mesh: grp: 1 (over z), comp: 2 (over y), row: 4 (over x, core).
Axes of the slice: x: 2, y: 2, z: 1, core: 2. Of those that a mesh axis runs over, the one named last changes fastest.
Arguments:
- points: bfloat16 [8192, 1024], P(('grp', 'row'))
- mu_init: float32 [2, 1024, 512], P(None, ('grp', 'comp'))
- logpi_init: float32 [2, 1024], P(None, ('grp', 'comp'))
- inv_temp: float32 [3], replicated
Outputs:
- output 1: float32 [2, 1024, 512], P(None, ('grp', 'comp'))
- output 2: float32 [2, 1024], P(None, ('grp', 'comp'))
- output 3: float32 [2, 8192], P(None, ('grp', 'row'))
All inputs are finite; a program needn't handle non-finite values.
Results may differ from a plain program's by a relative error of at most 0.001.
Values are sent between devices in bfloat16 or wider.
A program may use at most 1 GiB of HBM per device.

v0:
```python
import jax
import jax.numpy as jnp
from jax import lax
from jax.sharding import PartitionSpec as P

EPS_COUNT = 1e-6
PRIOR_ALPHA = 1e-3


def solution(mesh):
    comp_size = mesh.shape["comp"]
    row_size = mesh.shape["row"]

    def local_fit(x_local, mu_init, logpi_init, inv_temp):
        n_rows, full_dim = x_local.shape
        half_dim = full_dim // 2
        n_local = mu_init.shape[1]
        total_pts = n_rows * row_size
        total_comp = n_local * comp_size
        x_fits = jnp.transpose(x_local.reshape(n_rows, 2, half_dim), (1, 0, 2))
        sq_norm = jnp.sum(jnp.square(x_fits.astype(jnp.float32)), axis=2)
        mean_vecs = mu_init
        log_wts = logpi_init
        for sweep_idx in range(inv_temp.shape[0]):
            beta_t = inv_temp[sweep_idx]
            mu_sq = jnp.sum(mean_vecs * mean_vecs, axis=2)
            cross_dot = jnp.einsum("snh,skh->snk", x_fits, mean_vecs.astype(jnp.bfloat16), preferred_element_type=jnp.float32)
            logits = log_wts[:, None, :] - beta_t * (sq_norm[:, :, None] - 2.0 * cross_dot + mu_sq[:, None, :])
            row_max = lax.pmax(jnp.max(logits, axis=2), "comp")
            shifted = jnp.exp(logits - row_max[:, :, None])
            row_sum = lax.psum(jnp.sum(shifted, axis=2), "comp")
            log_norm = row_max + jnp.log(row_sum)
            resp_f = shifted / row_sum[:, :, None]
            counts = jnp.sum(resp_f, axis=1)
            stat_sum = jnp.einsum("snk,snh->skh", resp_f.astype(jnp.bfloat16), x_fits, preferred_element_type=jnp.float32)
            counts, stat_sum = lax.psum((counts, stat_sum), "row")
            mean_vecs = stat_sum / (counts[:, :, None] + EPS_COUNT)
            log_wts = jnp.log((counts + PRIOR_ALPHA) / (total_pts + total_comp * PRIOR_ALPHA))
        return mean_vecs, log_wts, log_norm

    return jax.shard_map(
        local_fit,
        mesh=mesh,
        in_specs=(P(("grp", "row"), None), P(None, ("grp", "comp"), None), P(None, ("grp", "comp")), P()),
        out_specs=(P(None, ("grp", "comp"), None), P(None, ("grp", "comp")), P(None, ("grp", "row"))),
        check_vma=False,
    )
```

profile of v0, /device:TPU:0, one launch (start us, length us, event | category | flops | bytes accessed | tf_op | source)
XLA Modules:
  0.0 282.0 jit_solution(18072243373159523039)
XLA Ops:
  7.2 1.4 fusion.29
  8.6 1.8 multiply_reduce_fusion.3
  10.4 3.1 %multiply_reduce_fusion = f32[2,2048]{1,0:T(2,128)S(1)} fusion(bf16[256,2,8,512]{3,2,1,0:T(8,128)(2,1)} %bitcast.64), kind=kLoop, calls=%fused_computation.10 | loop fusion | flops 6287360 | bytes 4210688 | tf_op jit(solution)/shard_map/reduce_sum | solution.py:21
  13.5 9.8 %fusion.30 = (f32[2,2048]{1,0:T(2,128)S(1)}, f32[2,2048,512]{1,2,0:T(8,128)}) fusion(f32[2,512]{1,0:T(2,128)S(1)} %multiply_reduce_fusion.3, f32[2,512,512]{2,1,0:T(8,128)} %param.5, bf16[256,2,8,512]{3,2,1,0:T(8,128)(2,1)} %bitcast.65, f32[2,2048]{1,0:T(2,128)S(1)} %multiply_reduce_fusion, f32[]{:T(128)} %bitcast, f32[2,512]{1,0:T(2,128)} %param.6), kind=kOutput, calls=%fused_computation.50 | convolution fusion | flops 2160586752 | bytes 14721028 | tf_op jit(solution)/shard_map/snh,skh->snk/dot_general | solution.py:27
  23.4 10.1 %pmax.21 = f32[2,2048]{1,0:T(2,128)S(1)} all-reduce(f32[2,2048]{1,0:T(2,128)S(1)} %get-tuple-element.12), channel_id=1, replica_groups=mesh['grp'=1,'comp'=2,'row'=4] {'comp'}, use_global_device_ids=true, to_apply=%region_3.0 | all-reduce | flops 4096 | bytes 32768 | tf_op jit(solution)/shard_map/pmax | solution.py:29
  33.5 4.5 %fusion.3 = f32[2,2048]{1,0:T(2,128)S(1)} fusion(f32[2,2048,512]{1,2,0:T(8,128)} %get-tuple-element.13, f32[2,2048]{1,0:T(2,128)S(1)} %pmax.21), kind=kLoop, calls=%fused_computation.12 | loop fusion | flops 4190208 | bytes 8421376 | tf_op jit(solution)/shard_map/reduce_sum | solution.py:31
  38.0 6.7 %psum.63 = f32[2,2048]{1,0:T(2,128)S(1)} all-reduce(f32[2,2048]{1,0:T(2,128)S(1)} %fusion.3), channel_id=1, replica_groups=mesh['grp'=1,'comp'=2,'row'=4] {'comp'}, use_global_device_ids=true, to_apply=%region_5.0 | all-reduce | flops 4096 | bytes 32768 | tf_op jit(solution)/shard_map/psum | solution.py:31
  44.7 8.2 %fusion.10 = f32[2,512,512]{2,1,0:T(8,128)} fusion(f32[2,2048,512]{1,2,0:T(8,128)} %get-tuple-element.13, f32[2,2048]{1,0:T(2,128)S(1)} %psum.63, f32[2,2048]{1,0:T(2,128)S(1)} %pmax.21, bf16[256,2,8,512]{3,2,1,0:T(8,128)(2,1)} %bitcast.66), kind=kOutput, calls=%fused_computation.20 | convolution fusion | flops 2153775104 | bytes 14712832 | tf_op jit(solution)/shard_map/snk,snh->skh/dot_general | solution.py:35
  53.0 4.2 %fusion.19 = f32[2,512]{1,0:T(2,128)S(1)} fusion(f32[2,2048]{1,0:T(2,128)S(1)} %psum.63, f32[2,2048,512]{1,2,0:T(8,128)} %get-tuple-element.13, f32[2,2048]{1,0:T(2,128)S(1)} %pmax.21), kind=kLoop, calls=%fused_computation.26 | loop fusion | flops 6290432 | bytes 8425472 | tf_op jit(solution)/shard_map/reduce_sum | solution.py:34
  57.2 6.2 %psum.64 = f32[2,512]{1,0:T(2,128)S(1)} all-reduce(f32[2,512]{1,0:T(2,128)S(1)} %fusion.19), channel_id=1, replica_groups=mesh['grp'=1,'comp'=2,'row'=4] {'row'}, use_global_device_ids=true, to_apply=%region_7.0 | all-reduce | flops 1024 | bytes 8192 | tf_op jit(solution)/shard_map/psum | solution.py:36
  63.5 36.8 %all-reduce.4.cloned.1.call-done = f32[2,512,512]{2,1,0:T(8,128)} async-done(((f32[2,512,512]{2,1,0:T(8,128)}), f32[2,512,512]{2,1,0:T(8,128)}) %all-reduce.4.cloned.1.call-update) | async-done | bytes 2097168 | tf_op jit(solution)/shard_map/psum | solution.py:36
  100.2 2.0 multiply_reduce_fusion.2
  102.2 9.9 %bitcast_reduce_fusion.1 = (f32[2,2048]{1,0:T(2,128)S(1)}, f32[2,512,2048]{2,1,0:T(8,128)}) fusion(f32[2,512]{1,0:T(2,128)S(1)} %multiply_reduce_fusion.2, bf16[256,2,8,512]{3,2,1,0:T(8,128)(2,1)} %bitcast.67, f32[2,512,512]{2,1,0:T(8,128)} %all-reduce.4.cloned.1.call-done, f32[2,512]{1,0:T(2,128)S(1)} %get-tuple-element.7, ...), kind=kOutput, calls=%fused_computation.4 | convolution fusion | flops 2161111040 | bytes 14725124 | tf_op jit(solution)/shard_map/snh,skh->snk/dot_general | solution.py:27
  112.1 8.1 %pmax.22 = f32[2,2048]{1,0:T(2,128)S(1)} all-reduce(f32[2,2048]{1,0:T(2,128)S(1)} %get-tuple-element.14), channel_id=1, replica_groups=mesh['grp'=1,'comp'=2,'row'=4] {'comp'}, use_global_device_ids=true, to_apply=%region_11.0 | all-reduce | flops 4096 | bytes 32768 | tf_op jit(solution)/shard_map/pmax | solution.py:29
  120.2 4.5 %fusion.5 = f32[2,2048]{1,0:T(2,128)S(1)} fusion(f32[2,512,2048]{2,1,0:T(8,128)} %get-tuple-element.15, f32[2,2048]{1,0:T(2,128)S(1)} %pmax.22), kind=kLoop, calls=%fused_computation.14 | loop fusion | flops 4190208 | bytes 8421376 | tf_op jit(solution)/shard_map/reduce_sum | solution.py:31
  124.7 7.2 %psum.66 = f32[2,2048]{1,0:T(2,128)S(1)} all-reduce(f32[2,2048]{1,0:T(2,128)S(1)} %fusion.5), channel_id=1, replica_groups=mesh['grp'=1,'comp'=2,'row'=4] {'comp'}, use_global_device_ids=true, to_apply=%region_13.0 | all-reduce | flops 4096 | bytes 32768 | tf_op jit(solution)/shard_map/psum | solution.py:31
  132.0 8.2 %fusion.9 = f32[2,512,512]{2,1,0:T(8,128)} fusion(f32[2,512,2048]{2,1,0:T(8,128)} %get-tuple-element.15, f32[2,2048]{1,0:T(2,128)S(1)} %psum.66, f32[2,2048]{1,0:T(2,128)S(1)} %pmax.22, bf16[256,2,8,512]{3,2,1,0:T(8,128)(2,1)} %bitcast.68), kind=kOutput, calls=%fused_computation.19 | convolution fusion | flops 2153775104 | bytes 14712832 | tf_op jit(solution)/shard_map/snk,snh->skh/dot_general | solution.py:35
  140.3 4.2 %fusion.17 = f32[2,512]{1,0:T(2,128)S(1)} fusion(f32[2,2048]{1,0:T(2,128)S(1)} %psum.66, f32[2,2048]{1,0:T(2,128)S(1)} %pmax.22, f32[2,512,2048]{2,1,0:T(8,128)} %get-tuple-element.15), kind=kLoop, calls=%fused_computation.25 | loop fusion | flops 6290432 | bytes 8425472 | tf_op jit(solution)/shard_map/reduce_sum | solution.py:34
  144.5 6.2 %psum.67 = f32[2,512]{1,0:T(2,128)S(1)} all-reduce(f32[2,512]{1,0:T(2,128)S(1)} %fusion.17), channel_id=1, replica_groups=mesh['grp'=1,'comp'=2,'row'=4] {'row'}, use_global_device_ids=true, to_apply=%region_15.0 | all-reduce | flops 1024 | bytes 8192 | tf_op jit(solution)/shard_map/psum | solution.py:36
  150.8 35.5 %all-reduce.6.cloned.1.call-done = f32[2,512,512]{2,1,0:T(8,128)} async-done(((f32[2,512,512]{2,1,0:T(8,128)}), f32[2,512,512]{2,1,0:T(8,128)}) %all-reduce.6.cloned.1.call-update) | async-done | bytes 2097168 | tf_op jit(solution)/shard_map/psum | solution.py:36
  186.3 2.0 multiply_reduce_fusion.1
  188.3 9.9 %bitcast_reduce_fusion = (f32[2,2048]{1,0:T(2,128)S(1)}, f32[2,512,2048]{2,1,0:T(8,128)}) fusion(f32[2,512]{1,0:T(2,128)S(1)} %multiply_reduce_fusion.1, bf16[256,2,8,512]{3,2,1,0:T(8,128)(2,1)} %bitcast.69, f32[2,512,512]{2,1,0:T(8,128)} %all-reduce.6.cloned.1.call-done, f32[2,512]{1,0:T(2,128)S(1)} %get-tuple-element.5, ...), kind=kOutput, calls=%fused_computation.1 | convolution fusion | flops 2161111040 | bytes 14725124 | tf_op jit(solution)/shard_map/snh,skh->snk/dot_general | solution.py:27
  198.1 8.1 %pmax.23 = f32[2,2048]{1,0:T(2,128)S(1)} all-reduce(f32[2,2048]{1,0:T(2,128)S(1)} %get-tuple-element.16), channel_id=1, replica_groups=mesh['grp'=1,'comp'=2,'row'=4] {'comp'}, use_global_device_ids=true, to_apply=%region_19.0 | all-reduce | flops 4096 | bytes 32768 | tf_op jit(solution)/shard_map/pmax | solution.py:29
  206.3 4.5 %fusion.7 = f32[2,2048]{1,0:T(2,128)S(1)} fusion(f32[2,512,2048]{2,1,0:T(8,128)} %get-tuple-element.17, f32[2,2048]{1,0:T(2,128)S(1)} %pmax.23), kind=kLoop, calls=%fused_computation.16 | loop fusion | flops 4190208 | bytes 8421376 | tf_op jit(solution)/shard_map/reduce_sum | solution.py:31
  210.8 7.2 %psum.69 = f32[2,2048]{1,0:T(2,128)S(1)} all-reduce(f32[2,2048]{1,0:T(2,128)S(1)} %fusion.7), channel_id=1, replica_groups=mesh['grp'=1,'comp'=2,'row'=4] {'comp'}, use_global_device_ids=true, to_apply=%region_21.0 | all-reduce | flops 4096 | bytes 32768 | tf_op jit(solution)/shard_map/psum | solution.py:31
  218.0 8.2 %fusion.8 = f32[2,512,512]{2,1,0:T(8,128)} fusion(f32[2,512,2048]{2,1,0:T(8,128)} %get-tuple-element.17, f32[2,2048]{1,0:T(2,128)S(1)} %psum.69, f32[2,2048]{1,0:T(2,128)S(1)} %pmax.23, bf16[256,2,8,512]{3,2,1,0:T(8,128)(2,1)} %bitcast.70), kind=kOutput, calls=%fused_computation.18 | convolution fusion | flops 2153775104 | bytes 14712832 | tf_op jit(solution)/shard_map/snk,snh->skh/dot_general | solution.py:35
  226.2 4.2 %fusion.14 = f32[2,512]{1,0:T(2,128)S(1)} fusion(f32[2,2048]{1,0:T(2,128)S(1)} %psum.69, f32[2,2048]{1,0:T(2,128)S(1)} %pmax.23, f32[2,512,2048]{2,1,0:T(8,128)} %get-tuple-element.17), kind=kLoop, calls=%fused_computation.24 | loop fusion | flops 6290432 | bytes 8425472 | tf_op jit(solution)/shard_map/reduce_sum | solution.py:34
  230.5 6.2 %psum.71 = f32[2,512]{1,0:T(2,128)S(1)} all-reduce(f32[2,512]{1,0:T(2,128)S(1)} %fusion.14), channel_id=1, replica_groups=mesh['grp'=1,'comp'=2,'row'=4] {'row'}, use_global_device_ids=true, to_apply=%region_24.0 | all-reduce | flops 1024 | bytes 8192 | tf_op jit(solution)/shard_map/psum | solution.py:36
  236.7 0.6 multiply_log_fusion
  237.3 0.6 log_add_fusion
  238.0 34.4 %all-reduce.8.cloned.1.call-done = f32[2,512,512]{2,1,0:T(8,128)} async-done(((f32[2,512,512]{2,1,0:T(8,128)}), f32[2,512,512]{2,1,0:T(8,128)}) %all-reduce.8.cloned.1.call-update) | async-done | bytes 2097168 | tf_op jit(solution)/shard_map/psum | solution.py:36
  272.3 3.1 %broadcast_divide_fusion = f32[2,512,512]{2,1,0:T(8,128)} fusion(f32[2,512,512]{2,1,0:T(8,128)} %all-reduce.8.cloned.1.call-done, f32[2,512]{1,0:T(2,128)S(1)} %get-tuple-element.4), kind=kLoop, calls=%fused_computation.36 | loop fusion | flops 524288 | bytes 4198400 | tf_op jit(solution)/shard_map/div | solution.py:37
  (8 shorter events, 0.2 us)
Async XLA Ops:
  7.2 93.1 %all-reduce.4.cloned.1.call-start = ((), (), s32[]{:S(2)}) async-start(), calls=%async_computation | async-start | bytes 4194304 | tf_op jit(solution)/shard_map/psum | solution.py:36
  52.9 133.4 %all-reduce.6.cloned.1.call-start = ((), (), s32[]{:S(2)}) async-start(), calls=%async_computation.1 | async-start | bytes 4194304 | tf_op jit(solution)/shard_map/psum | solution.py:36
  140.2 132.1 %all-reduce.8.cloned.1.call-start = ((), (), s32[]{:S(2)}) async-start(), calls=%async_computation.2 | async-start | bytes 4194304 | tf_op jit(solution)/shard_map/psum | solution.py:36
Sparse Core Ops, SparseCore 0:
  53.1 47.1 all-reduce.3
  140.3 45.9 all-reduce.5
  226.4 45.9 all-reduce.7
where the time goes:
time: 283 us; the launch traced here: 282 us
  waiting for transfers between devices  107 us (38%)
  blocking collectives  66.2 us (23%)
  matrix products  54.3 us (19%)
  other arithmetic  39.4 us (14%)
  between operations  13.8 us (5%)
    psum x3, waiting for transfers between devices, local_fit(): counts, stat_sum = lax.psum((counts, stat_sum), 'row')  107 us
    dot_general x3, matrix products, local_fit(): jnp.einsum('snh,skh->snk', x_fits, mean_vecs.astype(jnp.bfloat16), prefer...  29.6 us
    pmax x3, blocking collectives, local_fit(): row_max = lax.pmax(jnp.max(logits, axis=2), 'comp')  26.3 us
    dot_general x3, matrix products, local_fit(): jnp.einsum('snk,snh->skh', resp_f.astype(jnp.bfloat16), x_fits, preferred...  24.7 us
    psum x3, blocking collectives, local_fit(): row_sum = lax.psum(jnp.sum(shifted, axis=2), 'comp')  21.2 us
    psum x3, blocking collectives, local_fit(): counts, stat_sum = lax.psum((counts, stat_sum), 'row')  18.7 us
    reduce_sum x3, other arithmetic, local_fit(): row_sum = lax.psum(jnp.sum(shifted, axis=2), 'comp')  13.5 us
    reduce_sum x3, other arithmetic, local_fit(): counts = jnp.sum(resp_f, axis=1)  12.7 us
  transfers between devices with their start and end apart: 3, of which 3 were waited for; matrix products, arithmetic and copies ran while one was open for 5% of the time, Pallas kernels for 0%

commit v1 on v0

v1 whole, which is shorter than its diff:
```python
import jax
import jax.numpy as jnp
from jax import lax
from jax.experimental import pallas as pl
from jax.experimental.pallas import tpu as pltpu
from jax.sharding import PartitionSpec as P

EPS_COUNT = 1e-6
PRIOR_ALPHA = 1e-3

F32 = jnp.float32
BF16 = jnp.bfloat16
MESH = pl.DeviceIdType.MESH

SWEEPS = 3
HALF = 512
SHARD = 2048
ROWS = 8192
KC = 256
BLK = 256
NBLK = ROWS // BLK
GRP = 4
NGRP = NBLK // GRP
NCH = 16
Z = SHARD // 2 // NCH
OWN = 2 * SHARD
NQ = 4
QC = KC // NQ


def body(x_hbm, mu_hbm, lp_in, beta_ref,
         mu_out, lp_out, lse_out,
         xb, p_ref, rb, s_ref, nacc, mu_f, mu2, sqmu, lpb, sqx, lse_ref,
         st_own, st_rem, xin, lpbuf, lse_snd, lse_rcv,
         loc_sem, xs, xr, ys, yr, ds, dr, own_s, own_r,
         st_s, st_r, lps, lpr, ls_s, ls_r, fxs, fxr, fds, fdr, frs, frr, fl):
    comp = lax.axis_index("comp")
    row = lax.axis_index("row")
    side = row // 2
    core = row % 2
    sib = {"row": side * 2 + (1 - core)}
    ypt = {"comp": 1 - comp}
    ydg = {"comp": 1 - comp, "row": side * 2 + (1 - core)}
    xpt = {"row": (1 - side) * 2 + core}
    xdg = {"row": (1 - side) * 2 + (1 - core)}
    peers = (sib, ypt, ydg)

    barrier = pltpu.get_barrier_semaphore()
    for dev in (xpt, sib, ypt, ydg, xdg):
        pl.semaphore_signal(barrier, inc=1, device_id=dev, device_id_type=MESH)

    def remote(src, dst, ssem, rsem, dev):
        return pltpu.make_async_remote_copy(
            src_ref=src, dst_ref=dst, send_sem=ssem, recv_sem=rsem,
            device_id=dev, device_id_type=MESH)

    fit_cols = pl.ds(pl.multiple_of(side * HALF, HALF), HALF)
    oth_cols = pl.ds(pl.multiple_of((1 - side) * HALF, HALF), HALF)
    cbase = pl.multiple_of(core * KC, KC)

    def own_rows(c):
        return xb.at[pl.ds(pl.multiple_of(c * SHARD, SHARD), SHARD), :]

    ld_x = pltpu.make_async_copy(x_hbm.at[:, fit_cols], own_rows(core), loc_sem.at[0])
    ld_mu = pltpu.make_async_copy(mu_hbm.at[side, pl.ds(cbase, KC), :], mu_f, loc_sem.at[1])
    ld_mu.start()
    ld_x.start()

    def place(g, c, half, n):
        return xb.at[pl.ds(pl.multiple_of(OWN + g * (4 * Z) + c * (2 * Z) + half * Z, Z), n), :]

    def x_copy(g):
        src = x_hbm.at[pl.ds(pl.multiple_of(comp * (SHARD // 2) + g * Z, Z), Z), oth_cols]
        return remote(src, place(g, core, comp, Z), xs.at[g], xr.at[g], xpt)

    def y_copy(g):
        ref = place(g, core, comp, Z)
        return remote(ref, ref, ys.at[g], yr.at[g], ypt)

    def d_copy(g):
        ref = place(g, core, 0, 2 * Z)
        return remote(ref, ref, ds.at[g], dr.at[g], sib)

    own_copy = remote(x_hbm.at[:, fit_cols], own_rows(core), own_s, own_r, sib)

    pl.semaphore_wait(barrier, 5)
    own_copy.start()

    @pl.loop(0, NCH)
    def _(g):
        x_copy(g).start()

    def bc(row_vec):
        return jnp.transpose(jnp.broadcast_to(row_vec, (128, KC)))

    def set_means(mu):
        mu2[...] = mu.astype(BF16) * jnp.asarray(-2.0, BF16)
        sq = jnp.sum(mu * mu, axis=1, keepdims=True)
        sqmu[...] = jnp.broadcast_to(sq, (KC, 128))

    lpb[...] = bc(lp_in[pl.ds(side, 1), pl.ds(cbase, KC)])
    ld_mu.wait()
    set_means(mu_f[...])

    def point_sq(b):
        xf = xb[pl.ds(pl.multiple_of(b * BLK, BLK), BLK), :].astype(F32)
        sq = xf * xf
        part = (sq[:, 0:128] + sq[:, 128:256]) + (sq[:, 256:384] + sq[:, 384:512])
        rowv = jnp.sum(jnp.transpose(part), axis=0, keepdims=True)
        sqx[:, pl.ds(pl.multiple_of(b * BLK, BLK), BLK)] = rowv

    def estep(b, beta, par):
        xblk = xb[pl.ds(pl.multiple_of(b * BLK, BLK), BLK), :]
        a2 = lax.dot_general(mu2[...], xblk, (((1,), (1,)), ((), ())),
                             preferred_element_type=F32)
        sq = sqx[:, pl.ds(pl.multiple_of(b * BLK, BLK), BLK)]
        grp = b // GRP
        j = b % GRP
        for h in range(BLK // 128):
            cols = slice(h * 128, (h + 1) * 128)
            t = (a2[:, cols] + sq[:, cols]) + sqmu[...]
            logit = lpb[...] - beta * t
            m = jnp.max(logit, axis=0, keepdims=True)
            e = jnp.exp(logit - m)
            r = jnp.sum(e, axis=0, keepdims=True)
            p_ref[b, :, cols] = e
            st_own[par, grp, 0, j, :, cols] = m
            st_own[par, grp, 1, j, :, cols] = r

    def st_copy(grp, par, i):
        return remote(st_own.at[par, grp], st_rem.at[par, i, grp],
                      st_s.at[i, grp], st_r.at[par, i, grp], peers[i])

    def send_stats(grp, par):
        for i in range(3):
            st_copy(grp, par, i).start()

    def mstep(grp, par, first):
        for i in range(3):
            st_copy(grp, par, i).wait_recv()
            st_copy(grp, par, i).wait_send()
        st = [st_own[par, grp]] + [st_rem[par, i, grp] for i in range(3)]
        ms = [s[0] for s in st]
        rs = [s[1] for s in st]
        m = jnp.maximum(jnp.maximum(ms[0], ms[1]), jnp.maximum(ms[2], ms[3]))
        es = [jnp.exp(v - m) for v in ms]
        tot = (rs[0] * es[0] + rs[1] * es[1]) + (rs[2] * es[2] + rs[3] * es[3])
        scale = es[0] / tot
        lse = m + jnp.log(tot)
        cnt = None
        for j in range(GRP):
            lse_ref[:, pl.ds(pl.multiple_of((grp * GRP + j) * BLK, BLK), BLK)] = lse[j]
            rj = p_ref[grp * GRP + j] * scale[j]
            part = rj[:, 0:128] + rj[:, 128:256]
            cnt = part if cnt is None else cnt + part
            rb[:, j * BLK:(j + 1) * BLK] = rj.astype(BF16)
        nacc[...] += cnt
        rows = pl.ds(pl.multiple_of(grp * (GRP * BLK), GRP * BLK), GRP * BLK)
        s_ref[...] += jnp.dot(rb[...], xb[rows, :], preferred_element_type=F32)

    def zero_sums():
        nacc[...] = jnp.zeros_like(nacc)
        s_ref[...] = jnp.zeros_like(s_ref)

    def finish_sweep():
        n = jnp.sum(nacc[...], axis=1, keepdims=True)
        mu = s_ref[...] / (n + EPS_COUNT)
        mu_f[...] = mu
        lp = jnp.log((n + PRIOR_ALPHA) / (ROWS + 4 * KC * PRIOR_ALPHA))
        lpb[...] = jnp.broadcast_to(lp, (KC, 128))
        set_means(mu)

    zero_sums()
    beta0 = beta_ref[0]

    def first_blocks(c):
        @pl.loop(0, SHARD // BLK)
        def _(k):
            b = c * (SHARD // BLK) + k
            point_sq(b)
            estep(b, beta0, 0)

            @pl.when(k % GRP == GRP - 1)
            def _():
                send_stats(b // GRP, 0)

    ld_x.wait()
    first_blocks(core)
    own_copy.wait_recv()
    first_blocks(1 - core)

    @pl.loop(0, NCH + 4)
    def _(it):
        @pl.when(it < NCH)
        def _():
            x_copy(it).wait_recv()
            y_copy(it).start()

        @pl.when((it >= 3) & (it < NCH + 3))
        def _():
            y_copy(it - 3).wait_recv()
            d_copy(it - 3).start()

        @pl.when(it >= 4)
        def _():
            d_copy(it - 4).wait_recv()
            b = NBLK // 2 + it - 4
            point_sq(b)
            estep(b, beta0, 0)

            @pl.when(it % GRP == GRP - 1)
            def _():
                send_stats(b // GRP, 0)

        @pl.when((it < NCH) & (it % 4 == 2))
        def _():
            mstep(it // 4, 0, True)

        @pl.when((it >= 9) & (it % 4 == 1))
        def _():
            mstep(NGRP // 2 + (it - 9) // 4, 0, True)

    mstep(NGRP - 1, 0, True)
    finish_sweep()
    own_copy.wait_send()

    @pl.loop(0, NCH)
    def _(g):
        x_copy(g).wait_send()
        y_copy(g).wait_send()
        d_copy(g).wait_send()

    @pl.loop(1, SWEEPS)
    def _(t):
        par = t % 2
        beta = beta_ref[t]
        zero_sums()

        @pl.loop(0, NBLK)
        def _(b):
            estep(b, beta, par)

            @pl.when(b % GRP == GRP - 1)
            def _():
                send_stats(b // GRP, par)

        @pl.loop(0, NGRP)
        def _(grp):
            mstep(grp, par, False)

        finish_sweep()

    def fx_copy(q):
        rows = pl.ds(q * QC, QC)
        return remote(mu_f.at[rows, :], xin.at[rows, :], fxs.at[q], fxr.at[q], xpt)

    def out_rows(s, q, n):
        return mu_out.at[s, pl.ds(cbase + q * QC, n), :]

    def relay(q):
        return remote(xin.at[pl.ds(q * QC, QC), :], out_rows(1 - side, q, QC),
                      frs.at[q], frr.at[q], sib)

    def keep(q):
        return pltpu.make_async_copy(xin.at[pl.ds(q * QC, QC), :], out_rows(1 - side, q, QC),
                                     fl.at[1 + q])

    for q in range(NQ):
        fx_copy(q).start()
    to_sib = remote(mu_f, out_rows(side, 0, KC), fds, fdr, sib)
    to_sib.start()
    mine = pltpu.make_async_copy(mu_f, out_rows(side, 0, KC), fl.at[0])
    mine.start()

    slot = side * 2 + core
    lp_row = jnp.transpose(lpb[...])[0:1, :]
    lpbuf[slot] = lp_row
    lp_devs = (sib, xpt, xdg)

    def lp_copy(i):
        return remote(lpbuf.at[slot], lpbuf.at[slot], lps.at[i], lpr.at[i], lp_devs[i])

    halves = ([], [])
    for g in range(NCH):
        piece = lse_ref[:, pl.ds(pl.multiple_of(OWN + g * (4 * Z) + core * (2 * Z), 128), 128)]
        halves[0].append(piece[:, 0:Z])
        halves[1].append(piece[:, Z:2 * Z])
    lse_snd[...] = jnp.concatenate(halves[0] + halves[1], axis=1)
    lse_out[pl.ds(side, 1), :] = lse_ref[:, pl.ds(pl.multiple_of(core * SHARD, SHARD), SHARD)]
    lse_copy = remote(lse_snd, lse_rcv, ls_s, ls_r, xpt)
    lse_copy.start()
    for i in range(3):
        lp_copy(i).start()

    for q in range(NQ):
        fx_copy(q).wait_recv()
        relay(q).start()
        keep(q).start()

    lse_copy.wait()
    lse_out[pl.ds(1 - side, 1), :] = lse_rcv[...]
    for i in range(3):
        lp_copy(i).wait()
    for s in range(2):
        for c in range(2):
            lp_out[s:s + 1, c * KC:(c + 1) * KC] = lpbuf[s * 2 + c]
    mine.wait()
    to_sib.wait()
    for q in range(NQ):
        keep(q).wait()
        relay(q).wait()
        fx_copy(q).wait_send()


def solution(mesh):
    def local_fit(x_local, mu_init, logpi_init, inv_temp):
        dma = pltpu.SemaphoreType.DMA
        vmem = pl.BlockSpec(memory_space=pltpu.VMEM)
        hbm = pl.BlockSpec(memory_space=pl.ANY)
        return pl.pallas_call(
            body,
            out_shape=(
                jax.ShapeDtypeStruct(mu_init.shape, F32),
                jax.ShapeDtypeStruct(logpi_init.shape, F32),
                jax.ShapeDtypeStruct((2, x_local.shape[0]), F32),
            ),
            in_specs=[hbm, hbm, vmem, pl.BlockSpec(memory_space=pltpu.SMEM)],
            out_specs=(hbm, vmem, vmem),
            scratch_shapes=[
                pltpu.VMEM((ROWS, HALF), BF16),
                pltpu.VMEM((NBLK, KC, BLK), F32),
                pltpu.VMEM((KC, GRP * BLK), BF16),
                pltpu.VMEM((KC, HALF), F32),
                pltpu.VMEM((KC, 128), F32),
                pltpu.VMEM((KC, HALF), F32),
                pltpu.VMEM((KC, HALF), BF16),
                pltpu.VMEM((KC, 128), F32),
                pltpu.VMEM((KC, 128), F32),
                pltpu.VMEM((1, ROWS), F32),
                pltpu.VMEM((1, ROWS), F32),
                pltpu.VMEM((2, NGRP, 2, GRP, 1, BLK), F32),
                pltpu.VMEM((2, 3, NGRP, 2, GRP, 1, BLK), F32),
                pltpu.VMEM((KC, HALF), F32),
                pltpu.VMEM((4, 1, KC), F32),
                pltpu.VMEM((1, SHARD), F32),
                pltpu.VMEM((1, SHARD), F32),
                dma((2,)),
                dma((NCH,)), dma((NCH,)),
                dma((NCH,)), dma((NCH,)),
                dma((NCH,)), dma((NCH,)),
                dma, dma,
                dma((3, NGRP)), dma((2, 3, NGRP)),
                dma((3,)), dma((3,)),
                dma, dma,
                dma((NQ,)), dma((NQ,)),
                dma, dma,
                dma((NQ,)), dma((NQ,)),
                dma((NQ + 1,)),
            ],
            compiler_params=pltpu.CompilerParams(
                collective_id=0, has_side_effects=True,
                vmem_limit_bytes=56 * 1024 * 1024),
        )(x_local, mu_init, logpi_init, inv_temp)

    return jax.shard_map(
        local_fit,
        mesh=mesh,
        in_specs=(P(("grp", "row"), None), P(None, ("grp", "comp"), None), P(None, ("grp", "comp")), P()),
        out_specs=(P(None, ("grp", "comp"), None), P(None, ("grp", "comp")), P(None, ("grp", "row"))),
        check_vma=False,
    )
```

time: 283 us -> 94.1 us (0.33)
  waiting for transfers between devices: 107 us -> 0 us
  Pallas kernels: 0 us -> 89 us
  blocking collectives: 66.2 us -> 0 us
  matrix products: 54.3 us -> 0 us
  other arithmetic: 39.4 us -> 0 us
  between operations: 13.8 us -> 0.66 us
  local copies, waits for them, and re-layouts: 1.41 us -> 4.29 us
    psum x3 -> x0, waiting for transfers between devices: 107 us -> none  [local_fit(): counts, stat_sum = lax.psum((counts, stat_sum), 'row')]
    pallas_call x0 -> x1, Pallas kernels: none -> 89 us  [local_fit(): pl.pallas_call(body, out_shape=(jax.ShapeDtypeStruct(mu_init.shape, F32),...]
    dot_general x6 -> x0, matrix products: 54.3 us -> none  [the longest x3 29.6 us: local_fit(): jnp.einsum('snh,skh->snk', x_fits, mean_vecs.astype(jnp.bfloat16), prefer...]
    psum x6 -> x0, blocking collectives: 39.9 us -> none  [the longest x3 21.2 us: local_fit(): row_sum = lax.psum(jnp.sum(shifted, axis=2), 'comp')]
    reduce_sum x10 -> x0, other arithmetic: 35.1 us -> none  [the longest x3 13.5 us: local_fit(): row_sum = lax.psum(jnp.sum(shifted, axis=2), 'comp')]
    pmax x3 -> x0, blocking collectives: 26.3 us -> none  [local_fit(): row_max = lax.pmax(jnp.max(logits, axis=2), 'comp')]
    unnamed x0 -> x7, local copies, waits for them, and re-layouts: none -> 4.29 us
    div x1 -> x0, other arithmetic: 3.12 us -> none  [local_fit(): mean_vecs = stat_sum / (counts[:, :, None] + EPS_COUNT)]
  transfers between devices with their start and end apart: 3 -> 0, of which waited for: 3 -> 0; matrix products, arithmetic and copies ran while one was open for 5% -> 0% of each run, Pallas kernels for 0% -> 0%
where the time goes in v1:
time: 94.1 us; the launch traced here: 94 us
  Pallas kernels  89 us (95%)
  local copies, waits for them, and re-layouts  4.29 us (5%)
    pallas_call x1, Pallas kernels, local_fit(): pl.pallas_call(body, out_shape=(jax.ShapeDtypeStruct(mu_init.shape, F32),...  89 us
    unnamed x7, local copies, waits for them, and re-layouts  4.29 us

profile of v1, /device:TPU:0, one launch (start us, length us, event | category | flops | bytes accessed | tf_op | source)
XLA Modules:
  0.0 94.0 jit_solution(3351184198206962193)
XLA Ops:
  0.6 89.0 %shard_map.67 = (f32[2,512,512]{2,1,0:T(8,128)}, f32[2,512]{1,0:T(2,128)}, f32[2,2048]{1,0:T(2,128)}) custom-call(bf16[2048,1024]{1,0:T(8,128)(2,1)} %x_hbm.1, f32[2,512,512]{2,1,0:T(8,128)} %mu_hbm.1, f32[2,512]{1,0:T(2,128)} %lp_in.1, f32[3]{0:T(128)} %beta_ref.1), custom_call_target="tpu_custom_call" | custom-call | tf_op jit(solution)/shard_map/pallas_call | solution.py:320
  89.7 0.0 copy-start.1
  89.7 0.0 copy-start
  89.7 3.1 %copy.10 = f32[2,512,512]{2,1,0:T(8,128)} copy(f32[2,512,512]{2,1,0:T(8,128)} %get-tuple-element.6) | data formatting | bytes 4194304
  92.8 0.0 copy-done.1
  92.8 0.6 copy.11
  93.4 0.0 copy-done
  93.4 0.6 copy.12
Async XLA Ops:
  89.7 3.1 %copy-start.1 = (f32[2,512]{1,0:T(2,128)S(1)}, f32[2,512]{1,0:T(2,128)}, u32[]{:S(2)}) copy-start(f32[2,512]{1,0:T(2,128)} %get-tuple-element.7) | copy-start | bytes 12292
  89.7 3.7 %copy-start = (f32[2,2048]{1,0:T(2,128)S(1)}, f32[2,2048]{1,0:T(2,128)}, u32[]{:S(2)}) copy-start(f32[2,2048]{1,0:T(2,128)} %get-tuple-element.8) | copy-start | bytes 49156

commit v2 on v1

--- a/solution.py
+++ b/solution.py
@@ -23,6 +23,8 @@
 NGRP = NBLK // GRP
 NCH = 16
 Z = SHARD // 2 // NCH
+NOWN = 4
+PIECE = SHARD // NOWN
 OWN = 2 * SHARD
 NQ = 4
 QC = KC // NQ
@@ -30,7 +32,7 @@
 
 def body(x_hbm, mu_hbm, lp_in, beta_ref,
          mu_out, lp_out, lse_out,
-         xb, p_ref, rb, s_ref, nacc, mu_f, mu2, sqmu, lpb, sqx, lse_ref,
+         xb, xt_ref, p_ref, a0, a1, rb0, rb1, s_ref, nacc, mu_f, mu2, sqmu, lpb, sqx, lse_ref,
          st_own, st_rem, xin, lpbuf, lse_snd, lse_rcv,
          loc_sem, xs, xr, ys, yr, ds, dr, own_s, own_r,
          st_s, st_r, lps, lpr, ls_s, ls_r, fxs, fxr, fds, fdr, frs, frr, fl):
@@ -81,10 +83,14 @@
         ref = place(g, core, 0, 2 * Z)
         return remote(ref, ref, ds.at[g], dr.at[g], sib)
 
-    own_copy = remote(x_hbm.at[:, fit_cols], own_rows(core), own_s, own_r, sib)
+    def own_copy(k):
+        src = x_hbm.at[pl.ds(pl.multiple_of(k * PIECE, PIECE), PIECE), fit_cols]
+        dst = xb.at[pl.ds(pl.multiple_of(core * SHARD + k * PIECE, PIECE), PIECE), :]
+        return remote(src, dst, own_s.at[k], own_r.at[k], sib)
 
     pl.semaphore_wait(barrier, 5)
-    own_copy.start()
+    for k in range(NOWN):
+        own_copy(k).start()
 
     @pl.loop(0, NCH)
     def _(g):
@@ -102,23 +108,22 @@
     ld_mu.wait()
     set_means(mu_f[...])
 
-    def point_sq(b):
-        xf = xb[pl.ds(pl.multiple_of(b * BLK, BLK), BLK), :].astype(F32)
-        sq = xf * xf
-        part = (sq[:, 0:128] + sq[:, 128:256]) + (sq[:, 256:384] + sq[:, 384:512])
-        rowv = jnp.sum(jnp.transpose(part), axis=0, keepdims=True)
-        sqx[:, pl.ds(pl.multiple_of(b * BLK, BLK), BLK)] = rowv
-
-    def estep(b, beta, par):
-        xblk = xb[pl.ds(pl.multiple_of(b * BLK, BLK), BLK), :]
-        a2 = lax.dot_general(mu2[...], xblk, (((1,), (1,)), ((), ())),
-                             preferred_element_type=F32)
-        sq = sqx[:, pl.ds(pl.multiple_of(b * BLK, BLK), BLK)]
+    def prep(b):
+        xt = jnp.transpose(xb[pl.ds(pl.multiple_of(b * BLK, BLK), BLK), :])
+        xt_ref[b] = xt
+        xf = xt.astype(F32)
+        sqx[b] = jnp.sum(xf * xf, axis=0, keepdims=True)
+
+    def cross(b, a_ref):
+        a_ref[...] = jnp.dot(mu2[...], xt_ref[b], preferred_element_type=F32)
+
+    def soft(b, a_ref, beta, par):
+        sq = sqx[b]
         grp = b // GRP
         j = b % GRP
         for h in range(BLK // 128):
             cols = slice(h * 128, (h + 1) * 128)
-            t = (a2[:, cols] + sq[:, cols]) + sqmu[...]
+            t = (a_ref[:, cols] + sq[:, cols]) + sqmu[...]
             logit = lpb[...] - beta * t
             m = jnp.max(logit, axis=0, keepdims=True)
             e = jnp.exp(logit - m)
@@ -135,10 +140,12 @@
         for i in range(3):
             st_copy(grp, par, i).start()
 
-    def mstep(grp, par, first):
+    def wait_stats(grp, par):
         for i in range(3):
             st_copy(grp, par, i).wait_recv()
             st_copy(grp, par, i).wait_send()
+
+    def resp(grp, par, rb):
         st = [st_own[par, grp]] + [st_rem[par, i, grp] for i in range(3)]
         ms = [s[0] for s in st]
         rs = [s[1] for s in st]
@@ -147,16 +154,22 @@
         tot = (rs[0] * es[0] + rs[1] * es[1]) + (rs[2] * es[2] + rs[3] * es[3])
         scale = es[0] / tot
         lse = m + jnp.log(tot)
-        cnt = None
+        cnt = nacc[...]
         for j in range(GRP):
             lse_ref[:, pl.ds(pl.multiple_of((grp * GRP + j) * BLK, BLK), BLK)] = lse[j]
             rj = p_ref[grp * GRP + j] * scale[j]
-            part = rj[:, 0:128] + rj[:, 128:256]
-            cnt = part if cnt is None else cnt + part
+            cnt = cnt + (rj[:, 0:128] + rj[:, 128:256])
             rb[:, j * BLK:(j + 1) * BLK] = rj.astype(BF16)
-        nacc[...] += cnt
+        nacc[...] = cnt
+
+    def gather(grp, rb):
         rows = pl.ds(pl.multiple_of(grp * (GRP * BLK), GRP * BLK), GRP * BLK)
         s_ref[...] += jnp.dot(rb[...], xb[rows, :], preferred_element_type=F32)
+
+    def mstep(grp, par):
+        wait_stats(grp, par)
+        resp(grp, par, rb0)
+        gather(grp, rb0)
 
     def zero_sums():
         nacc[...] = jnp.zeros_like(nacc)
@@ -173,21 +186,16 @@
     zero_sums()
     beta0 = beta_ref[0]
 
-    def first_blocks(c):
-        @pl.loop(0, SHARD // BLK)
-        def _(k):
-            b = c * (SHARD // BLK) + k
-            point_sq(b)
-            estep(b, beta0, 0)
-
-            @pl.when(k % GRP == GRP - 1)
-            def _():
-                send_stats(b // GRP, 0)
+    def first_block(b):
+        prep(b)
+        cross(b, a0)
+        soft(b, a0, beta0, 0)
+
+        @pl.when(b % GRP == GRP - 1)
+        def _():
+            send_stats(b // GRP, 0)
 
     ld_x.wait()
-    first_blocks(core)
-    own_copy.wait_recv()
-    first_blocks(1 - core)
 
     @pl.loop(0, NCH + 4)
     def _(it):
@@ -201,28 +209,31 @@
             y_copy(it - 3).wait_recv()
             d_copy(it - 3).start()
 
+        @pl.when((it < NCH) & (it // 8 != core) & (it % 2 == 0))
+        def _():
+            own_copy((it % 8) // 2).wait_recv()
+
+        @pl.when(it < NCH)
+        def _():
+            first_block(it)
+
         @pl.when(it >= 4)
         def _():
             d_copy(it - 4).wait_recv()
-            b = NBLK // 2 + it - 4
-            point_sq(b)
-            estep(b, beta0, 0)
-
-            @pl.when(it % GRP == GRP - 1)
-            def _():
-                send_stats(b // GRP, 0)
-
-        @pl.when((it < NCH) & (it % 4 == 2))
-        def _():
-            mstep(it // 4, 0, True)
+            first_block(NBLK // 2 + it - 4)
+
+        @pl.when((it >= 6) & (it % 4 == 2))
+        def _():
+            mstep((it - 6) // 4, 0)
 
         @pl.when((it >= 9) & (it % 4 == 1))
         def _():
-            mstep(NGRP // 2 + (it - 9) // 4, 0, True)
-
-    mstep(NGRP - 1, 0, True)
+            mstep(NGRP // 2 + (it - 9) // 4, 0)
+
+    mstep(NGRP - 1, 0)
     finish_sweep()
-    own_copy.wait_send()
+    for k in range(NOWN):
+        own_copy(k).wait_send()
 
     @pl.loop(0, NCH)
     def _(g):
@@ -235,19 +246,37 @@
         par = t % 2
         beta = beta_ref[t]
         zero_sums()
-
-        @pl.loop(0, NBLK)
-        def _(b):
-            estep(b, beta, par)
-
-            @pl.when(b % GRP == GRP - 1)
+        cross(0, a0)
+
+        @pl.loop(0, NBLK // 2)
+        def _(i):
+            b = 2 * i
+            cross(b + 1, a1)
+            soft(b, a0, beta, par)
+            cross((b + 2) % NBLK, a0)
+            soft(b + 1, a1, beta, par)
+
+            @pl.when(i % 2 == 1)
             def _():
-                send_stats(b // GRP, par)
-
-        @pl.loop(0, NGRP)
-        def _(grp):
-            mstep(grp, par, False)
-
+                send_stats(i // 2, par)
+
+        wait_stats(0, par)
+        resp(0, par, rb0)
+
+        @pl.loop(0, NGRP // 2 - 1)
+        def _(i):
+            g = 2 * i
+            wait_stats(g + 1, par)
+            resp(g + 1, par, rb1)
+            gather(g, rb0)
+            wait_stats(g + 2, par)
+            resp(g + 2, par, rb0)
+            gather(g + 1, rb1)
+
+        wait_stats(NGRP - 1, par)
+        resp(NGRP - 1, par, rb1)
+        gather(NGRP - 2, rb0)
+        gather(NGRP - 1, rb1)
         finish_sweep()
 
     def fx_copy(q):
@@ -328,7 +357,10 @@
             out_specs=(hbm, vmem, vmem),
             scratch_shapes=[
                 pltpu.VMEM((ROWS, HALF), BF16),
+                pltpu.VMEM((NBLK, HALF, BLK), BF16),
                 pltpu.VMEM((NBLK, KC, BLK), F32),
+                pltpu.VMEM((KC, BLK), F32), pltpu.VMEM((KC, BLK), F32),
+                pltpu.VMEM((KC, GRP * BLK), BF16),
                 pltpu.VMEM((KC, GRP * BLK), BF16),
                 pltpu.VMEM((KC, HALF), F32),
                 pltpu.VMEM((KC, 128), F32),
@@ -336,7 +368,7 @@
                 pltpu.VMEM((KC, HALF), BF16),
                 pltpu.VMEM((KC, 128), F32),
                 pltpu.VMEM((KC, 128), F32),
-                pltpu.VMEM((1, ROWS), F32),
+                pltpu.VMEM((NBLK, 1, BLK), F32),
                 pltpu.VMEM((1, ROWS), F32),
                 pltpu.VMEM((2, NGRP, 2, GRP, 1, BLK), F32),
                 pltpu.VMEM((2, 3, NGRP, 2, GRP, 1, BLK), F32),
@@ -348,7 +380,7 @@
                 dma((NCH,)), dma((NCH,)),
                 dma((NCH,)), dma((NCH,)),
                 dma((NCH,)), dma((NCH,)),
-                dma, dma,
+                dma((NOWN,)), dma((NOWN,)),
                 dma((3, NGRP)), dma((2, 3, NGRP)),
                 dma((3,)), dma((3,)),
                 dma, dma,

time: 94.1 us -> 83.8 us (0.89)
  Pallas kernels: 89 us -> 78.7 us
    pallas_call x1, Pallas kernels: 89 us -> 78.7 us  [local_fit(): pl.pallas_call(body, out_shape=(jax.ShapeDtypeStruct(mu_init.shape, F32),...]
where the time goes in v2:
time: 83.8 us; the launch traced here: 83.6 us
  Pallas kernels  78.7 us (94%)
  local copies, waits for them, and re-layouts  4.29 us (5%)
    pallas_call x1, Pallas kernels, local_fit(): pl.pallas_call(body, out_shape=(jax.ShapeDtypeStruct(mu_init.shape, F32),...  78.7 us
    unnamed x7, local copies, waits for them, and re-layouts  4.29 us

profile of v2, /device:TPU:0, one launch (start us, length us, event | category | flops | bytes accessed | tf_op | source)
XLA Modules:
  0.0 83.6 jit_solution(16770946632122654267)
XLA Ops:
  0.6 78.7 %shard_map.67 = (f32[2,512,512]{2,1,0:T(8,128)}, f32[2,512]{1,0:T(2,128)}, f32[2,2048]{1,0:T(2,128)}) custom-call(bf16[2048,1024]{1,0:T(8,128)(2,1)} %x_hbm.1, f32[2,512,512]{2,1,0:T(8,128)} %mu_hbm.1, f32[2,512]{1,0:T(2,128)} %lp_in.1, f32[3]{0:T(128)} %beta_ref.1), custom_call_target="tpu_custom_call" | custom-call | tf_op jit(solution)/shard_map/pallas_call | solution.py:349
  79.3 0.0 copy-start.1
  79.3 0.0 copy-start
  79.3 3.1 %copy.10 = f32[2,512,512]{2,1,0:T(8,128)} copy(f32[2,512,512]{2,1,0:T(8,128)} %get-tuple-element.6) | data formatting | bytes 4194304
  82.4 0.0 copy-done.1
  82.4 0.6 copy.11
  83.0 0.0 copy-done
  83.0 0.6 copy.12
Async XLA Ops:
  79.3 3.1 %copy-start.1 = (f32[2,512]{1,0:T(2,128)S(1)}, f32[2,512]{1,0:T(2,128)}, u32[]{:S(2)}) copy-start(f32[2,512]{1,0:T(2,128)} %get-tuple-element.7) | copy-start | bytes 12292
  79.3 3.7 %copy-start = (f32[2,2048]{1,0:T(2,128)S(1)}, f32[2,2048]{1,0:T(2,128)}, u32[]{:S(2)}) copy-start(f32[2,2048]{1,0:T(2,128)} %get-tuple-element.8) | copy-start | bytes 49156

commit v3 on v2

--- a/solution.py
+++ b/solution.py
@@ -33,9 +33,9 @@
 def body(x_hbm, mu_hbm, lp_in, beta_ref,
          mu_out, lp_out, lse_out,
          xb, xt_ref, p_ref, a0, a1, rb0, rb1, s_ref, nacc, mu_f, mu2, sqmu, lpb, sqx, lse_ref,
-         st_own, st_rem, xin, lpbuf, lse_snd, lse_rcv,
+         st_own, st_rem, lpbuf, lse_snd, lse_rcv,
          loc_sem, xs, xr, ys, yr, ds, dr, own_s, own_r,
-         st_s, st_r, lps, lpr, ls_s, ls_r, fxs, fxr, fds, fdr, frs, frr, fl):
+         st_s, st_r, lps, lpr, ls_s, ls_r, fxs, fxr, fds, fdr, frs, frr):
     comp = lax.axis_index("comp")
     row = lax.axis_index("row")
     side = row // 2
@@ -222,14 +222,16 @@
             d_copy(it - 4).wait_recv()
             first_block(NBLK // 2 + it - 4)
 
-        @pl.when((it >= 6) & (it % 4 == 2))
-        def _():
-            mstep((it - 6) // 4, 0)
-
-        @pl.when((it >= 9) & (it % 4 == 1))
-        def _():
-            mstep(NGRP // 2 + (it - 9) // 4, 0)
-
+        @pl.when((it >= 10) & (it % 4 == 2))
+        def _():
+            mstep((it - 10) // 4, 0)
+
+        @pl.when((it >= 13) & (it % 4 == 1))
+        def _():
+            mstep(NGRP // 2 + (it - 13) // 4, 0)
+
+    mstep(NGRP // 2 - 1, 0)
+    mstep(NGRP - 2, 0)
     mstep(NGRP - 1, 0)
     finish_sweep()
     for k in range(NOWN):
@@ -279,35 +281,30 @@
         gather(NGRP - 1, rb1)
         finish_sweep()
 
+    def block(s, q, n):
+        return mu_out.at[s, pl.ds(cbase + q * QC, n), :]
+
     def fx_copy(q):
-        rows = pl.ds(q * QC, QC)
-        return remote(mu_f.at[rows, :], xin.at[rows, :], fxs.at[q], fxr.at[q], xpt)
-
-    def out_rows(s, q, n):
-        return mu_out.at[s, pl.ds(cbase + q * QC, n), :]
+        ref = block(side, q, QC)
+        return remote(ref, ref, fxs.at[q], fxr.at[q], xpt)
 
     def relay(q):
-        return remote(xin.at[pl.ds(q * QC, QC), :], out_rows(1 - side, q, QC),
-                      frs.at[q], frr.at[q], sib)
-
-    def keep(q):
-        return pltpu.make_async_copy(xin.at[pl.ds(q * QC, QC), :], out_rows(1 - side, q, QC),
-                                     fl.at[1 + q])
+        ref = block(1 - side, q, QC)
+        return remote(ref, ref, frs.at[q], frr.at[q], sib)
+
+    mu_out[side, pl.ds(cbase, KC), :] = mu_f[...]
+    to_sib = remote(block(side, 0, KC), block(side, 0, KC), fds, fdr, sib)
+
+    slot = side * 2 + core
+    lpbuf[slot] = jnp.transpose(lpb[...])[0:1, :]
+    lp_devs = (sib, xpt, xdg)
+
+    def lp_copy(i):
+        return remote(lpbuf.at[slot], lpbuf.at[slot], lps.at[i], lpr.at[i], lp_devs[i])
 
     for q in range(NQ):
         fx_copy(q).start()
-    to_sib = remote(mu_f, out_rows(side, 0, KC), fds, fdr, sib)
     to_sib.start()
-    mine = pltpu.make_async_copy(mu_f, out_rows(side, 0, KC), fl.at[0])
-    mine.start()
-
-    slot = side * 2 + core
-    lp_row = jnp.transpose(lpb[...])[0:1, :]
-    lpbuf[slot] = lp_row
-    lp_devs = (sib, xpt, xdg)
-
-    def lp_copy(i):
-        return remote(lpbuf.at[slot], lpbuf.at[slot], lps.at[i], lpr.at[i], lp_devs[i])
 
     halves = ([], [])
     for g in range(NCH):
@@ -320,12 +317,6 @@
     lse_copy.start()
     for i in range(3):
         lp_copy(i).start()
-
-    for q in range(NQ):
-        fx_copy(q).wait_recv()
-        relay(q).start()
-        keep(q).start()
-
     lse_copy.wait()
     lse_out[pl.ds(1 - side, 1), :] = lse_rcv[...]
     for i in range(3):
@@ -333,10 +324,13 @@
     for s in range(2):
         for c in range(2):
             lp_out[s:s + 1, c * KC:(c + 1) * KC] = lpbuf[s * 2 + c]
-    mine.wait()
+
+    for q in range(NQ):
+        fx_copy(q).wait_recv()
+        relay(q).start()
+
     to_sib.wait()
     for q in range(NQ):
-        keep(q).wait()
         relay(q).wait()
         fx_copy(q).wait_send()
 
@@ -345,16 +339,15 @@
     def local_fit(x_local, mu_init, logpi_init, inv_temp):
         dma = pltpu.SemaphoreType.DMA
         vmem = pl.BlockSpec(memory_space=pltpu.VMEM)
-        hbm = pl.BlockSpec(memory_space=pl.ANY)
-        return pl.pallas_call(
+        hbm = pl.BlockSpec(memory_space=pltpu.HBM)
+        outs = [jax.ShapeDtypeStruct(mu_init.shape, F32),
+                jax.ShapeDtypeStruct(logpi_init.shape, F32),
+                jax.ShapeDtypeStruct((2, x_local.shape[0]), F32)]
+        res = pl.pallas_call(
             body,
-            out_shape=(
-                jax.ShapeDtypeStruct(mu_init.shape, F32),
-                jax.ShapeDtypeStruct(logpi_init.shape, F32),
-                jax.ShapeDtypeStruct((2, x_local.shape[0]), F32),
-            ),
+            out_shape=tuple(pltpu.VMEM(o.shape, o.dtype) for o in outs),
             in_specs=[hbm, hbm, vmem, pl.BlockSpec(memory_space=pltpu.SMEM)],
-            out_specs=(hbm, vmem, vmem),
+            out_specs=(vmem, vmem, vmem),
             scratch_shapes=[
                 pltpu.VMEM((ROWS, HALF), BF16),
                 pltpu.VMEM((NBLK, HALF, BLK), BF16),
@@ -372,7 +365,6 @@
                 pltpu.VMEM((1, ROWS), F32),
                 pltpu.VMEM((2, NGRP, 2, GRP, 1, BLK), F32),
                 pltpu.VMEM((2, 3, NGRP, 2, GRP, 1, BLK), F32),
-                pltpu.VMEM((KC, HALF), F32),
                 pltpu.VMEM((4, 1, KC), F32),
                 pltpu.VMEM((1, SHARD), F32),
                 pltpu.VMEM((1, SHARD), F32),
@@ -387,12 +379,12 @@
                 dma((NQ,)), dma((NQ,)),
                 dma, dma,
                 dma((NQ,)), dma((NQ,)),
-                dma((NQ + 1,)),
             ],
             compiler_params=pltpu.CompilerParams(
                 collective_id=0, has_side_effects=True,
                 vmem_limit_bytes=56 * 1024 * 1024),
         )(x_local, mu_init, logpi_init, inv_temp)
+        return tuple(res)
 
     return jax.shard_map(
         local_fit,

time: 83.8 us -> 80.5 us (0.961)
  local copies, waits for them, and re-layouts: 4.29 us -> 2.52 us
  Pallas kernels: 78.7 us -> 77.2 us
    unnamed x7 -> x3, local copies, waits for them, and re-layouts: 4.29 us -> 2.52 us
    pallas_call x1, Pallas kernels: 78.7 us -> 77.2 us  [local_fit(): pl.pallas_call(body, out_shape=tuple((pltpu.VMEM(o.shape, o.dtype) for o...]
where the time goes in v3:
time: 80.5 us; the launch traced here: 80.4 us
  Pallas kernels  77.2 us (96%)
  local copies, waits for them, and re-layouts  2.52 us (3%)
    pallas_call x1, Pallas kernels, local_fit(): pl.pallas_call(body, out_shape=tuple((pltpu.VMEM(o.shape, o.dtype) for o...  77.2 us
    unnamed x3, local copies, waits for them, and re-layouts  2.52 us

profile of v3, /device:TPU:0, one launch (start us, length us, event | category | flops | bytes accessed | tf_op | source)
XLA Modules:
  0.0 80.4 jit_solution(14846645418666934995)
XLA Ops:
  0.6 77.2 %shard_map.67 = (f32[2,512,512]{2,1,0:T(8,128)S(1)}, f32[2,512]{1,0:T(2,128)S(1)}, f32[2,2048]{1,0:T(2,128)S(1)}) custom-call(bf16[2048,1024]{1,0:T(8,128)(2,1)} %x_hbm.1, f32[2,512,512]{2,1,0:T(8,128)} %mu_hbm.1, f32[2,512]{1,0:T(2,128)} %lp_in.1, f32[3]{0:T(128)} %beta_ref.1), custom_call_target="tpu_custom_call" | custom-call | tf_op jit(solution)/shard_map/pallas_call | solution.py:346
  77.8 1.3 %copy.10 = f32[2,512,512]{2,1,0:T(8,128)} copy(f32[2,512,512]{2,1,0:T(8,128)S(1)} %get-tuple-element.3) | data formatting | bytes 4194304
  79.2 0.6 copy.11
  79.8 0.6 copy.12

commit v4 on v3

--- a/solution.py
+++ b/solution.py
@@ -32,7 +32,7 @@
 
 def body(x_hbm, mu_hbm, lp_in, beta_ref,
          mu_out, lp_out, lse_out,
-         xb, xt_ref, p_ref, a0, a1, rb0, rb1, s_ref, nacc, mu_f, mu2, sqmu, lpb, sqx, lse_ref,
+         xb, xt_ref, p_ref, a0, a1, rb0, rb1, s_ref, nacc, mu_f, mu2, sqmu, lpb, sqx, mx_ref, lse_ref,
          st_own, st_rem, lpbuf, lse_snd, lse_rcv,
          loc_sem, xs, xr, ys, yr, ds, dr, own_s, own_r,
          st_s, st_r, lps, lpr, ls_s, ls_r, fxs, fxr, fds, fdr, frs, frr):
@@ -72,27 +72,30 @@
         return xb.at[pl.ds(pl.multiple_of(OWN + g * (4 * Z) + c * (2 * Z) + half * Z, Z), n), :]
 
     def x_copy(g):
-        src = x_hbm.at[pl.ds(pl.multiple_of(comp * (SHARD // 2) + g * Z, Z), Z), oth_cols]
-        return remote(src, place(g, core, comp, Z), xs.at[g], xr.at[g], xpt)
+        extra = g // NCH
+        g0 = g - extra
+        half = comp + extra * (1 - 2 * comp)
+        src = x_hbm.at[pl.ds(pl.multiple_of(half * (SHARD // 2) + g0 * Z, Z), Z), oth_cols]
+        return remote(src, place(g0, core, half, Z), xs, xr.at[g], xpt)
 
     def y_copy(g):
         ref = place(g, core, comp, Z)
-        return remote(ref, ref, ys.at[g], yr.at[g], ypt)
+        return remote(ref, ref, ys, yr.at[g], ypt)
 
     def d_copy(g):
         ref = place(g, core, 0, 2 * Z)
-        return remote(ref, ref, ds.at[g], dr.at[g], sib)
+        return remote(ref, ref, ds, dr.at[g], sib)
 
     def own_copy(k):
         src = x_hbm.at[pl.ds(pl.multiple_of(k * PIECE, PIECE), PIECE), fit_cols]
         dst = xb.at[pl.ds(pl.multiple_of(core * SHARD + k * PIECE, PIECE), PIECE), :]
-        return remote(src, dst, own_s.at[k], own_r.at[k], sib)
+        return remote(src, dst, own_s, own_r.at[k], sib)
 
     pl.semaphore_wait(barrier, 5)
     for k in range(NOWN):
         own_copy(k).start()
 
-    @pl.loop(0, NCH)
+    @pl.loop(0, NCH + 1)
     def _(g):
         x_copy(g).start()
 
@@ -129,31 +132,31 @@
             e = jnp.exp(logit - m)
             r = jnp.sum(e, axis=0, keepdims=True)
             p_ref[b, :, cols] = e
-            st_own[par, grp, 0, j, :, cols] = m
-            st_own[par, grp, 1, j, :, cols] = r
+            mx_ref[b, :, cols] = m
+            st_own[par, grp, j, :, cols] = m + jnp.log(r)
 
     def st_copy(grp, par, i):
-        return remote(st_own.at[par, grp], st_rem.at[par, i, grp],
-                      st_s.at[i, grp], st_r.at[par, i, grp], peers[i])
+        return remote(st_own.at[par, grp], st_rem.at[par, grp, i],
+                      st_s.at[grp], st_r.at[par, grp], peers[i])
 
     def send_stats(grp, par):
         for i in range(3):
             st_copy(grp, par, i).start()
 
     def wait_stats(grp, par):
-        for i in range(3):
-            st_copy(grp, par, i).wait_recv()
-            st_copy(grp, par, i).wait_send()
+        three = st_rem.at[par, grp]
+        both = remote(three, three, st_s.at[grp], st_r.at[par, grp], sib)
+        both.wait_recv()
+        both.wait_send()
 
     def resp(grp, par, rb):
-        st = [st_own[par, grp]] + [st_rem[par, i, grp] for i in range(3)]
-        ms = [s[0] for s in st]
-        rs = [s[1] for s in st]
-        m = jnp.maximum(jnp.maximum(ms[0], ms[1]), jnp.maximum(ms[2], ms[3]))
-        es = [jnp.exp(v - m) for v in ms]
-        tot = (rs[0] * es[0] + rs[1] * es[1]) + (rs[2] * es[2] + rs[3] * es[3])
-        scale = es[0] / tot
-        lse = m + jnp.log(tot)
+        st = [st_own[par, grp]] + [st_rem[par, grp, i] for i in range(3)]
+        top = jnp.maximum(jnp.maximum(st[0], st[1]), jnp.maximum(st[2], st[3]))
+        es = [jnp.exp(v - top) for v in st]
+        tot = (es[0] + es[1]) + (es[2] + es[3])
+        lse = top + jnp.log(tot)
+        first = pl.multiple_of(grp * GRP, GRP)
+        scale = jnp.exp(mx_ref[pl.ds(first, GRP)] - top) / tot
         cnt = nacc[...]
         for j in range(GRP):
             lse_ref[:, pl.ds(pl.multiple_of((grp * GRP + j) * BLK, BLK), BLK)] = lse[j]
@@ -199,16 +202,22 @@
 
     @pl.loop(0, NCH + 4)
     def _(it):
-        @pl.when(it < NCH)
+        @pl.when(it < NCH - 1)
         def _():
             x_copy(it).wait_recv()
             y_copy(it).start()
 
-        @pl.when((it >= 3) & (it < NCH + 3))
+        @pl.when((it >= 3) & (it < NCH + 2))
         def _():
             y_copy(it - 3).wait_recv()
             d_copy(it - 3).start()
 
+        @pl.when(it == NCH + 2)
+        def _():
+            x_copy(NCH - 1).wait_recv()
+            x_copy(NCH).wait_recv()
+            d_copy(NCH - 1).start()
+
         @pl.when((it < NCH) & (it // 8 != core) & (it % 2 == 0))
         def _():
             own_copy((it % 8) // 2).wait_recv()
@@ -222,26 +231,27 @@
             d_copy(it - 4).wait_recv()
             first_block(NBLK // 2 + it - 4)
 
-        @pl.when((it >= 10) & (it % 4 == 2))
-        def _():
-            mstep((it - 10) // 4, 0)
-
-        @pl.when((it >= 13) & (it % 4 == 1))
-        def _():
-            mstep(NGRP // 2 + (it - 13) // 4, 0)
+        @pl.when((it >= 8) & (it < NCH + 4) & (it % 4 == 0))
+        def _():
+            mstep((it - 8) // 4, 0)
+
+        @pl.when((it >= 14) & (it % 4 == 2))
+        def _():
+            mstep(NGRP // 2 + (it - 14) // 4, 0)
 
     mstep(NGRP // 2 - 1, 0)
     mstep(NGRP - 2, 0)
     mstep(NGRP - 1, 0)
     finish_sweep()
-    for k in range(NOWN):
-        own_copy(k).wait_send()
-
-    @pl.loop(0, NCH)
-    def _(g):
-        x_copy(g).wait_send()
-        y_copy(g).wait_send()
-        d_copy(g).wait_send()
+
+    def all_sent(n, sem):
+        ref = xb.at[pl.ds(0, n), :]
+        remote(ref, ref, sem, own_r.at[0], sib).wait_send()
+
+    all_sent(SHARD, own_s)
+    all_sent((NCH + 1) * Z, xs)
+    all_sent((NCH - 1) * Z, ys)
+    all_sent(NCH * 2 * Z, ds)
 
     @pl.loop(1, SWEEPS)
     def _(t):
@@ -286,11 +296,11 @@
 
     def fx_copy(q):
         ref = block(side, q, QC)
-        return remote(ref, ref, fxs.at[q], fxr.at[q], xpt)
+        return remote(ref, ref, fxs, fxr.at[q], xpt)
 
     def relay(q):
         ref = block(1 - side, q, QC)
-        return remote(ref, ref, frs.at[q], frr.at[q], sib)
+        return remote(ref, ref, frs, frr, sib)
 
     mu_out[side, pl.ds(cbase, KC), :] = mu_f[...]
     to_sib = remote(block(side, 0, KC), block(side, 0, KC), fds, fdr, sib)
@@ -300,11 +310,8 @@
     lp_devs = (sib, xpt, xdg)
 
     def lp_copy(i):
-        return remote(lpbuf.at[slot], lpbuf.at[slot], lps.at[i], lpr.at[i], lp_devs[i])
-
-    for q in range(NQ):
-        fx_copy(q).start()
-    to_sib.start()
+        return remote(lpbuf.at[slot], lpbuf.at[slot], lps, lpr, lp_devs[i])
+
 
     halves = ([], [])
     for g in range(NCH):
@@ -317,10 +324,12 @@
     lse_copy.start()
     for i in range(3):
         lp_copy(i).start()
+    for q in range(NQ):
+        fx_copy(q).start()
+    to_sib.start()
     lse_copy.wait()
     lse_out[pl.ds(1 - side, 1), :] = lse_rcv[...]
-    for i in range(3):
-        lp_copy(i).wait()
+    remote(lpbuf.at[pl.ds(0, 3)], lpbuf.at[pl.ds(0, 3)], lps, lpr, sib).wait()
     for s in range(2):
         for c in range(2):
             lp_out[s:s + 1, c * KC:(c + 1) * KC] = lpbuf[s * 2 + c]
@@ -330,9 +339,8 @@
         relay(q).start()
 
     to_sib.wait()
-    for q in range(NQ):
-        relay(q).wait()
-        fx_copy(q).wait_send()
+    remote(block(1 - side, 0, KC), block(1 - side, 0, KC), frs, frr, sib).wait()
+    remote(block(side, 0, KC), block(side, 0, KC), fxs, frr, xpt).wait_send()
 
 
 def solution(mesh):
@@ -362,23 +370,24 @@
                 pltpu.VMEM((KC, 128), F32),
                 pltpu.VMEM((KC, 128), F32),
                 pltpu.VMEM((NBLK, 1, BLK), F32),
+                pltpu.VMEM((NBLK, 1, BLK), F32),
                 pltpu.VMEM((1, ROWS), F32),
-                pltpu.VMEM((2, NGRP, 2, GRP, 1, BLK), F32),
-                pltpu.VMEM((2, 3, NGRP, 2, GRP, 1, BLK), F32),
+                pltpu.VMEM((2, NGRP, GRP, 1, BLK), F32),
+                pltpu.VMEM((2, NGRP, 3, GRP, 1, BLK), F32),
                 pltpu.VMEM((4, 1, KC), F32),
                 pltpu.VMEM((1, SHARD), F32),
                 pltpu.VMEM((1, SHARD), F32),
                 dma((2,)),
-                dma((NCH,)), dma((NCH,)),
-                dma((NCH,)), dma((NCH,)),
-                dma((NCH,)), dma((NCH,)),
-                dma((NOWN,)), dma((NOWN,)),
-                dma((3, NGRP)), dma((2, 3, NGRP)),
-                dma((3,)), dma((3,)),
+                dma, dma((NCH + 1,)),
+                dma, dma((NCH - 1,)),
+                dma, dma((NCH,)),
+                dma, dma((NOWN,)),
+                dma((NGRP,)), dma((2, NGRP)),
                 dma, dma,
-                dma((NQ,)), dma((NQ,)),
                 dma, dma,
-                dma((NQ,)), dma((NQ,)),
+                dma, dma((NQ,)),
+                dma, dma,
+                dma, dma,
             ],
             compiler_params=pltpu.CompilerParams(
                 collective_id=0, has_side_effects=True,

time: 80.5 us -> 77.2 us (0.959)
  Pallas kernels: 77.2 us -> 73.9 us
    pallas_call x1, Pallas kernels: 77.2 us -> 73.9 us  [local_fit(): pl.pallas_call(body, out_shape=tuple((pltpu.VMEM(o.shape, o.dtype) for o...]
where the time goes in v4:
time: 77.2 us; the launch traced here: 77.1 us
  Pallas kernels  73.9 us (96%)
  local copies, waits for them, and re-layouts  2.52 us (3%)
    pallas_call x1, Pallas kernels, local_fit(): pl.pallas_call(body, out_shape=tuple((pltpu.VMEM(o.shape, o.dtype) for o...  73.9 us
    unnamed x3, local copies, waits for them, and re-layouts  2.52 us

profile of v4, /device:TPU:0, one launch (start us, length us, event | category | flops | bytes accessed | tf_op | source)
XLA Modules:
  0.0 77.1 jit_solution(13411578593203427280)
XLA Ops:
  0.6 73.9 %shard_map.67 = (f32[2,512,512]{2,1,0:T(8,128)S(1)}, f32[2,512]{1,0:T(2,128)S(1)}, f32[2,2048]{1,0:T(2,128)S(1)}) custom-call(bf16[2048,1024]{1,0:T(8,128)(2,1)} %x_hbm.1, f32[2,512,512]{2,1,0:T(8,128)} %mu_hbm.1, f32[2,512]{1,0:T(2,128)} %lp_in.1, f32[3]{0:T(128)} %beta_ref.1), custom_call_target="tpu_custom_call" | custom-call | tf_op jit(solution)/shard_map/pallas_call | solution.py:354
  74.6 1.3 %copy.10 = f32[2,512,512]{2,1,0:T(8,128)} copy(f32[2,512,512]{2,1,0:T(8,128)S(1)} %get-tuple-element.3) | data formatting | bytes 4194304
  75.9 0.6 copy.11
  76.5 0.6 copy.12

commit v5 on v4

--- a/solution.py
+++ b/solution.py
@@ -212,7 +212,7 @@
             y_copy(it - 3).wait_recv()
             d_copy(it - 3).start()
 
-        @pl.when(it == NCH + 2)
+        @pl.when(it == NCH + 1)
         def _():
             x_copy(NCH - 1).wait_recv()
             x_copy(NCH).wait_recv()
@@ -231,16 +231,16 @@
             d_copy(it - 4).wait_recv()
             first_block(NBLK // 2 + it - 4)
 
-        @pl.when((it >= 8) & (it < NCH + 4) & (it % 4 == 0))
+        @pl.when((it >= 8) & (it < NCH) & (it % 4 == 0))
         def _():
             mstep((it - 8) // 4, 0)
 
-        @pl.when((it >= 14) & (it % 4 == 2))
+        @pl.when((it >= 14) & (it < NCH) & (it % 4 == 2))
         def _():
             mstep(NGRP // 2 + (it - 14) // 4, 0)
 
-    mstep(NGRP // 2 - 1, 0)
-    mstep(NGRP - 2, 0)
+    for g in (2, 3, 5, 6):
+        mstep(g, 0)
     mstep(NGRP - 1, 0)
     finish_sweep()
 
@@ -258,37 +258,18 @@
         par = t % 2
         beta = beta_ref[t]
         zero_sums()
-        cross(0, a0)
-
-        @pl.loop(0, NBLK // 2)
+        @pl.loop(0, NBLK // 8)
         def _(i):
-            b = 2 * i
-            cross(b + 1, a1)
-            soft(b, a0, beta, par)
-            cross((b + 2) % NBLK, a0)
-            soft(b + 1, a1, beta, par)
-
-            @pl.when(i % 2 == 1)
-            def _():
-                send_stats(i // 2, par)
-
-        wait_stats(0, par)
-        resp(0, par, rb0)
-
-        @pl.loop(0, NGRP // 2 - 1)
-        def _(i):
-            g = 2 * i
-            wait_stats(g + 1, par)
-            resp(g + 1, par, rb1)
-            gather(g, rb0)
-            wait_stats(g + 2, par)
-            resp(g + 2, par, rb0)
-            gather(g + 1, rb1)
-
-        wait_stats(NGRP - 1, par)
-        resp(NGRP - 1, par, rb1)
-        gather(NGRP - 2, rb0)
-        gather(NGRP - 1, rb1)
+            for k in range(8):
+                b = 8 * i + k
+                soft(b, jnp.dot(mu2[...], xt_ref[b], preferred_element_type=F32), beta, par)
+            for g in range(8 // GRP):
+                send_stats(i * (8 // GRP) + g, par)
+
+        for g in range(NGRP):
+            wait_stats(g, par)
+            resp(g, par, (rb0, rb1)[g % 2])
+            gather(g, (rb0, rb1)[g % 2])
         finish_sweep()
 
     def block(s, q, n):

time: 77.2 us -> 70.7 us (0.916)
  Pallas kernels: 73.9 us -> 67.4 us
    pallas_call x1, Pallas kernels: 73.9 us -> 67.4 us  [local_fit(): pl.pallas_call(body, out_shape=tuple((pltpu.VMEM(o.shape, o.dtype) for o...]
where the time goes in v5:
time: 70.7 us; the launch traced here: 70.5 us
  Pallas kernels  67.4 us (95%)
  local copies, waits for them, and re-layouts  2.52 us (4%)
    pallas_call x1, Pallas kernels, local_fit(): pl.pallas_call(body, out_shape=tuple((pltpu.VMEM(o.shape, o.dtype) for o...  67.4 us
    unnamed x3, local copies, waits for them, and re-layouts  2.52 us

profile of v5, /device:TPU:0, one launch (start us, length us, event | category | flops | bytes accessed | tf_op | source)
XLA Modules:
  0.0 70.5 jit_solution(771324941187073308)
XLA Ops:
  0.6 67.4 %shard_map.67 = (f32[2,512,512]{2,1,0:T(8,128)S(1)}, f32[2,512]{1,0:T(2,128)S(1)}, f32[2,2048]{1,0:T(2,128)S(1)}) custom-call(bf16[2048,1024]{1,0:T(8,128)(2,1)} %x_hbm.1, f32[2,512,512]{2,1,0:T(8,128)} %mu_hbm.1, f32[2,512]{1,0:T(2,128)} %lp_in.1, f32[3]{0:T(128)} %beta_ref.1), custom_call_target="tpu_custom_call" | custom-call | tf_op jit(solution)/shard_map/pallas_call | solution.py:335
  68.0 1.3 %copy.10 = f32[2,512,512]{2,1,0:T(8,128)} copy(f32[2,512,512]{2,1,0:T(8,128)S(1)} %get-tuple-element.3) | data formatting | bytes 4194304
  69.3 0.6 copy.11
  69.9 0.6 copy.12

commit v6 on v5

--- a/solution.py
+++ b/solution.py
@@ -14,6 +14,7 @@
 
 SWEEPS = 3
 HALF = 512
+HH = HALF // 2
 SHARD = 2048
 ROWS = 8192
 KC = 256
@@ -23,6 +24,7 @@
 NGRP = NBLK // GRP
 NCH = 16
 Z = SHARD // 2 // NCH
+PRE = 4
 NOWN = 4
 PIECE = SHARD // NOWN
 OWN = 2 * SHARD
@@ -30,9 +32,9 @@
 QC = KC // NQ
 
 
-def body(x_hbm, mu_hbm, lp_in, beta_ref,
+def body(x_hbm, mu_hbm, lp_hbm, beta_hbm,
          mu_out, lp_out, lse_out,
-         xb, xt_ref, p_ref, a0, a1, rb0, rb1, s_ref, nacc, mu_f, mu2, sqmu, lpb, sqx, mx_ref, lse_ref,
+         xb, xt_ref, p_ref, rb, xpre, lp_in, beta_ref, s_ref, nacc, inv_n, mu_f, mu2, sqmu, lpb, sqx, mx_ref, lse_ref,
          st_own, st_rem, lpbuf, lse_snd, lse_rcv,
          loc_sem, xs, xr, ys, yr, ds, dr, own_s, own_r,
          st_s, st_r, lps, lpr, ls_s, ls_r, fxs, fxr, fds, fdr, frs, frr):
@@ -65,7 +67,15 @@
 
     ld_x = pltpu.make_async_copy(x_hbm.at[:, fit_cols], own_rows(core), loc_sem.at[0])
     ld_mu = pltpu.make_async_copy(mu_hbm.at[side, pl.ds(cbase, KC), :], mu_f, loc_sem.at[1])
+    ld_pre = pltpu.make_async_copy(
+        x_hbm.at[pl.ds(pl.multiple_of(comp * (SHARD // 2), PRE * Z), PRE * Z), oth_cols],
+        xpre, loc_sem.at[2])
+    ld_lp = pltpu.make_async_copy(lp_hbm, lp_in, loc_sem.at[3])
+    ld_beta = pltpu.make_async_copy(beta_hbm, beta_ref, loc_sem.at[4])
+    ld_pre.start()
     ld_mu.start()
+    ld_lp.start()
+    ld_beta.start()
     ld_x.start()
 
     def place(g, c, half, n):
@@ -92,24 +102,30 @@
         return remote(src, dst, own_s, own_r.at[k], sib)
 
     pl.semaphore_wait(barrier, 5)
+    ld_pre.wait()
+    for g in range(PRE):
+        remote(xpre.at[pl.ds(g * Z, Z), :], place(g, core, comp, Z), xs, xr.at[g], xpt).start()
     for k in range(NOWN):
         own_copy(k).start()
 
-    @pl.loop(0, NCH + 1)
+    @pl.loop(PRE, NCH + 1)
     def _(g):
         x_copy(g).start()
 
     def bc(row_vec):
         return jnp.transpose(jnp.broadcast_to(row_vec, (128, KC)))
 
-    def set_means(mu):
-        mu2[...] = mu.astype(BF16) * jnp.asarray(-2.0, BF16)
-        sq = jnp.sum(mu * mu, axis=1, keepdims=True)
-        sqmu[...] = jnp.broadcast_to(sq, (KC, 128))
-
+    def set_means(h, mu):
+        mu2[:, h * HH:(h + 1) * HH] = mu.astype(BF16) * jnp.asarray(-2.0, BF16)
+        sq = jnp.broadcast_to(jnp.sum(mu * mu, axis=1, keepdims=True), (KC, 128))
+        sqmu[...] = sq if h == 0 else sqmu[...] + sq
+
+    ld_lp.wait()
+    ld_beta.wait()
     lpb[...] = bc(lp_in[pl.ds(side, 1), pl.ds(cbase, KC)])
     ld_mu.wait()
-    set_means(mu_f[...])
+    for h in range(2):
+        set_means(h, mu_f[:, h * HH:(h + 1) * HH])
 
     def prep(b):
         xt = jnp.transpose(xb[pl.ds(pl.multiple_of(b * BLK, BLK), BLK), :])
@@ -117,16 +133,16 @@
         xf = xt.astype(F32)
         sqx[b] = jnp.sum(xf * xf, axis=0, keepdims=True)
 
-    def cross(b, a_ref):
-        a_ref[...] = jnp.dot(mu2[...], xt_ref[b], preferred_element_type=F32)
-
-    def soft(b, a_ref, beta, par):
+    def cross(b):
+        return jnp.dot(mu2[...], xt_ref[b], preferred_element_type=F32)
+
+    def soft(b, a2, beta, par):
         sq = sqx[b]
         grp = b // GRP
         j = b % GRP
         for h in range(BLK // 128):
             cols = slice(h * 128, (h + 1) * 128)
-            t = (a_ref[:, cols] + sq[:, cols]) + sqmu[...]
+            t = (a2[:, cols] + sq[:, cols]) + sqmu[...]
             logit = lpb[...] - beta * t
             m = jnp.max(logit, axis=0, keepdims=True)
             e = jnp.exp(logit - m)
@@ -149,7 +165,7 @@
         both.wait_recv()
         both.wait_send()
 
-    def resp(grp, par, rb):
+    def resp(grp, par):
         st = [st_own[par, grp]] + [st_rem[par, grp, i] for i in range(3)]
         top = jnp.maximum(jnp.maximum(st[0], st[1]), jnp.maximum(st[2], st[3]))
         es = [jnp.exp(v - top) for v in st]
@@ -162,43 +178,58 @@
             lse_ref[:, pl.ds(pl.multiple_of((grp * GRP + j) * BLK, BLK), BLK)] = lse[j]
             rj = p_ref[grp * GRP + j] * scale[j]
             cnt = cnt + (rj[:, 0:128] + rj[:, 128:256])
-            rb[:, j * BLK:(j + 1) * BLK] = rj.astype(BF16)
+            rb[grp, :, j * BLK:(j + 1) * BLK] = rj.astype(BF16)
         nacc[...] = cnt
 
-    def gather(grp, rb):
+    def gather(grp, h):
         rows = pl.ds(pl.multiple_of(grp * (GRP * BLK), GRP * BLK), GRP * BLK)
-        s_ref[...] += jnp.dot(rb[...], xb[rows, :], preferred_element_type=F32)
+        s_ref[h] += jnp.dot(rb[grp], xb[rows, h * HH:(h + 1) * HH], preferred_element_type=F32)
 
     def mstep(grp, par):
         wait_stats(grp, par)
-        resp(grp, par, rb0)
-        gather(grp, rb0)
+        resp(grp, par)
+        gather(grp, 0)
+        gather(grp, 1)
 
     def zero_sums():
         nacc[...] = jnp.zeros_like(nacc)
         s_ref[...] = jnp.zeros_like(s_ref)
 
-    def finish_sweep():
+    def finish_counts():
         n = jnp.sum(nacc[...], axis=1, keepdims=True)
-        mu = s_ref[...] / (n + EPS_COUNT)
-        mu_f[...] = mu
         lp = jnp.log((n + PRIOR_ALPHA) / (ROWS + 4 * KC * PRIOR_ALPHA))
         lpb[...] = jnp.broadcast_to(lp, (KC, 128))
-        set_means(mu)
+        inv_n[...] = jnp.broadcast_to(1.0 / (n + EPS_COUNT), (KC, 128))
+
+    def finish_means(h):
+        inv = inv_n[...]
+        mu = s_ref[h] * jnp.concatenate([inv, inv], axis=1)
+        mu_out[side, pl.ds(cbase, KC), h * HH:(h + 1) * HH] = mu
+        set_means(h, mu)
 
     zero_sums()
     beta0 = beta_ref[0]
 
     def first_block(b):
         prep(b)
-        cross(b, a0)
-        soft(b, a0, beta0, 0)
+        soft(b, cross(b), beta0, 0)
 
         @pl.when(b % GRP == GRP - 1)
         def _():
             send_stats(b // GRP, 0)
 
+    def own_block(n):
+        @pl.when((n >= 8) & (n % 2 == 0))
+        def _():
+            own_copy((n - 8) // 2).wait_recv()
+
+        first_block((core * 8 + n) % 16)
+
     ld_x.wait()
+
+    @pl.loop(0, 4)
+    def _(n):
+        own_block(n)
 
     @pl.loop(0, NCH + 4)
     def _(it):
@@ -218,31 +249,30 @@
             x_copy(NCH).wait_recv()
             d_copy(NCH - 1).start()
 
-        @pl.when((it < NCH) & (it // 8 != core) & (it % 2 == 0))
-        def _():
-            own_copy((it % 8) // 2).wait_recv()
-
-        @pl.when(it < NCH)
-        def _():
-            first_block(it)
+        @pl.when(it < 4)
+        def _():
+            @pl.loop(0, 2)
+            def _(k):
+                own_block(4 + 2 * it + k)
+
+        @pl.when((it >= 4) & (it < 8))
+        def _():
+            own_block(8 + it)
 
         @pl.when(it >= 4)
         def _():
             d_copy(it - 4).wait_recv()
             first_block(NBLK // 2 + it - 4)
 
-        @pl.when((it >= 8) & (it < NCH) & (it % 4 == 0))
-        def _():
-            mstep((it - 8) // 4, 0)
-
-        @pl.when((it >= 14) & (it < NCH) & (it % 4 == 2))
-        def _():
-            mstep(NGRP // 2 + (it - 14) // 4, 0)
-
-    for g in (2, 3, 5, 6):
-        mstep(g, 0)
+        @pl.when((it >= 9) & (it < 15))
+        def _():
+            mstep(it - 9, 0)
+
+    mstep(NGRP - 2, 0)
     mstep(NGRP - 1, 0)
-    finish_sweep()
+    finish_counts()
+    for h in range(2):
+        finish_means(h)
 
     def all_sent(n, sem):
         ref = xb.at[pl.ds(0, n), :]
@@ -252,6 +282,43 @@
     all_sent((NCH + 1) * Z, xs)
     all_sent((NCH - 1) * Z, ys)
     all_sent(NCH * 2 * Z, ds)
+
+    def block(s, q):
+        return mu_out.at[s, pl.ds(cbase + (q % 2) * (KC // 2), KC // 2), pl.ds((q // 2) * HH, HH)]
+
+    def whole(s):
+        return mu_out.at[s, pl.ds(cbase, KC), :]
+
+    def fx_copy(q):
+        ref = block(side, q)
+        return remote(ref, ref, fxs, fxr.at[q], xpt)
+
+    def relay(q):
+        ref = block(1 - side, q)
+        return remote(ref, ref, frs, frr, sib)
+
+    def send_half(h):
+        for q in (2 * h, 2 * h + 1):
+            fx_copy(q).start()
+        ref = mu_out.at[side, pl.ds(cbase, KC), pl.ds(h * HH, HH)]
+        remote(ref, ref, fds, fdr, sib).start()
+
+    slot = side * 2 + core
+    lp_devs = (sib, xpt, xdg)
+    lse_copy = remote(lse_snd, lse_rcv, ls_s, ls_r, xpt)
+
+    def send_small():
+        lpbuf[slot] = jnp.transpose(lpb[...])[0:1, :]
+        halves = ([], [])
+        for g in range(NCH):
+            piece = lse_ref[:, pl.ds(pl.multiple_of(OWN + g * (4 * Z) + core * (2 * Z), 128), 128)]
+            halves[0].append(piece[:, 0:Z])
+            halves[1].append(piece[:, Z:2 * Z])
+        lse_snd[...] = jnp.concatenate(halves[0] + halves[1], axis=1)
+        lse_out[pl.ds(side, 1), :] = lse_ref[:, pl.ds(pl.multiple_of(core * SHARD, SHARD), SHARD)]
+        lse_copy.start()
+        for i in range(3):
+            remote(lpbuf.at[slot], lpbuf.at[slot], lps, lpr, lp_devs[i]).start()
 
     @pl.loop(1, SWEEPS)
     def _(t):
@@ -262,52 +329,30 @@
         def _(i):
             for k in range(8):
                 b = 8 * i + k
-                soft(b, jnp.dot(mu2[...], xt_ref[b], preferred_element_type=F32), beta, par)
+                soft(b, cross(b), beta, par)
             for g in range(8 // GRP):
                 send_stats(i * (8 // GRP) + g, par)
 
         for g in range(NGRP):
             wait_stats(g, par)
-            resp(g, par, (rb0, rb1)[g % 2])
-            gather(g, (rb0, rb1)[g % 2])
-        finish_sweep()
-
-    def block(s, q, n):
-        return mu_out.at[s, pl.ds(cbase + q * QC, n), :]
-
-    def fx_copy(q):
-        ref = block(side, q, QC)
-        return remote(ref, ref, fxs, fxr.at[q], xpt)
-
-    def relay(q):
-        ref = block(1 - side, q, QC)
-        return remote(ref, ref, frs, frr, sib)
-
-    mu_out[side, pl.ds(cbase, KC), :] = mu_f[...]
-    to_sib = remote(block(side, 0, KC), block(side, 0, KC), fds, fdr, sib)
-
-    slot = side * 2 + core
-    lpbuf[slot] = jnp.transpose(lpb[...])[0:1, :]
-    lp_devs = (sib, xpt, xdg)
-
-    def lp_copy(i):
-        return remote(lpbuf.at[slot], lpbuf.at[slot], lps, lpr, lp_devs[i])
-
-
-    halves = ([], [])
-    for g in range(NCH):
-        piece = lse_ref[:, pl.ds(pl.multiple_of(OWN + g * (4 * Z) + core * (2 * Z), 128), 128)]
-        halves[0].append(piece[:, 0:Z])
-        halves[1].append(piece[:, Z:2 * Z])
-    lse_snd[...] = jnp.concatenate(halves[0] + halves[1], axis=1)
-    lse_out[pl.ds(side, 1), :] = lse_ref[:, pl.ds(pl.multiple_of(core * SHARD, SHARD), SHARD)]
-    lse_copy = remote(lse_snd, lse_rcv, ls_s, ls_r, xpt)
-    lse_copy.start()
-    for i in range(3):
-        lp_copy(i).start()
-    for q in range(NQ):
-        fx_copy(q).start()
-    to_sib.start()
+            resp(g, par)
+            gather(g, 0)
+        finish_counts()
+        finish_means(0)
+
+        @pl.when(t == SWEEPS - 1)
+        def _():
+            send_small()
+            send_half(0)
+
+        for g in range(NGRP):
+            gather(g, 1)
+        finish_means(1)
+
+        @pl.when(t == SWEEPS - 1)
+        def _():
+            send_half(1)
+
     lse_copy.wait()
     lse_out[pl.ds(1 - side, 1), :] = lse_rcv[...]
     remote(lpbuf.at[pl.ds(0, 3)], lpbuf.at[pl.ds(0, 3)], lps, lpr, sib).wait()
@@ -319,9 +364,18 @@
         fx_copy(q).wait_recv()
         relay(q).start()
 
-    to_sib.wait()
-    remote(block(1 - side, 0, KC), block(1 - side, 0, KC), frs, frr, sib).wait()
-    remote(block(side, 0, KC), block(side, 0, KC), fxs, frr, xpt).wait_send()
+    remote(whole(side), whole(side), fds, fdr, sib).wait()
+    remote(whole(1 - side), whole(1 - side), frs, frr, sib).wait()
+    remote(whole(side), whole(side), fxs, frr, xpt).wait_send()
+
+
+def write_out(mu_v, lp_v, lse_v, mu_o, lp_o, lse_o, sem):
+    pairs = ((mu_v, mu_o), (lp_v, lp_o), (lse_v, lse_o))
+    copies = [pltpu.make_async_copy(src, dst, sem.at[i]) for i, (src, dst) in enumerate(pairs)]
+    for c in copies:
+        c.start()
+    for c in copies:
+        c.wait()
 
 
 def solution(mesh):
@@ -335,16 +389,18 @@
         res = pl.pallas_call(
             body,
             out_shape=tuple(pltpu.VMEM(o.shape, o.dtype) for o in outs),
-            in_specs=[hbm, hbm, vmem, pl.BlockSpec(memory_space=pltpu.SMEM)],
+            in_specs=[hbm] * 4,
             out_specs=(vmem, vmem, vmem),
             scratch_shapes=[
                 pltpu.VMEM((ROWS, HALF), BF16),
                 pltpu.VMEM((NBLK, HALF, BLK), BF16),
                 pltpu.VMEM((NBLK, KC, BLK), F32),
-                pltpu.VMEM((KC, BLK), F32), pltpu.VMEM((KC, BLK), F32),
-                pltpu.VMEM((KC, GRP * BLK), BF16),
-                pltpu.VMEM((KC, GRP * BLK), BF16),
-                pltpu.VMEM((KC, HALF), F32),
+                pltpu.VMEM((NGRP, KC, GRP * BLK), BF16),
+                pltpu.VMEM((PRE * Z, HALF), BF16),
+                pltpu.VMEM((2, 2 * KC), F32),
+                pltpu.SMEM((SWEEPS,), F32),
+                pltpu.VMEM((2, KC, HH), F32),
+                pltpu.VMEM((KC, 128), F32),
                 pltpu.VMEM((KC, 128), F32),
                 pltpu.VMEM((KC, HALF), F32),
                 pltpu.VMEM((KC, HALF), BF16),
@@ -358,7 +414,7 @@
                 pltpu.VMEM((4, 1, KC), F32),
                 pltpu.VMEM((1, SHARD), F32),
                 pltpu.VMEM((1, SHARD), F32),
-                dma((2,)),
+                dma((5,)),
                 dma, dma((NCH + 1,)),
                 dma, dma((NCH - 1,)),
                 dma, dma((NCH,)),
@@ -374,7 +430,13 @@
                 collective_id=0, has_side_effects=True,
                 vmem_limit_bytes=56 * 1024 * 1024),
         )(x_local, mu_init, logpi_init, inv_temp)
-        return tuple(res)
+        return pl.pallas_call(
+            write_out,
+            out_shape=tuple(outs),
+            in_specs=[vmem] * 3,
+            out_specs=(hbm,) * 3,
+            scratch_shapes=[dma((3,))],
+        )(*[pltpu.with_memory_space_constraint(r, pltpu.VMEM) for r in res])
 
     return jax.shard_map(
         local_fit,

time: 70.7 us -> 70.9 us (level)
  Pallas kernels: 67.4 us -> 70.2 us
  local copies, waits for them, and re-layouts: 2.52 us -> 0 us
    unnamed x3 -> x0, local copies, waits for them, and re-layouts: 2.52 us -> none
    pallas_call x1, Pallas kernels: 67.4 us -> 68.8 us  [local_fit(): pl.pallas_call(body, out_shape=tuple((pltpu.VMEM(o.shape, o.dtype) for o...]
    pallas_call x0 -> x1, Pallas kernels: none -> 1.35 us  [local_fit(): pl.pallas_call(write_out, out_shape=tuple(outs), in_specs=[vmem] * 3, out...]
where the time goes in v6:
time: 70.9 us; the launch traced here: 70.8 us
  Pallas kernels  70.2 us (99%)
    pallas_call x1, Pallas kernels, local_fit(): pl.pallas_call(body, out_shape=tuple((pltpu.VMEM(o.shape, o.dtype) for o...  68.8 us

profile of v6, /device:TPU:0, one launch (start us, length us, event | category | flops | bytes accessed | tf_op | source)
XLA Modules:
  0.0 70.8 jit_solution(13918593768497373031)
XLA Ops:
  0.6 68.8 %shard_map.67 = (f32[2,512,512]{2,1,0:T(8,128)S(1)}, f32[2,512]{1,0:T(2,128)S(1)}, f32[2,2048]{1,0:T(2,128)S(1)}) custom-call(bf16[2048,1024]{1,0:T(8,128)(2,1)} %x_hbm.1, f32[2,512,512]{2,1,0:T(8,128)} %mu_hbm.1, f32[2,512]{1,0:T(2,128)} %lp_hbm.1, f32[3]{0:T(128)} %beta_hbm.1), custom_call_target="tpu_custom_call" | custom-call | tf_op jit(solution)/shard_map/pallas_call | solution.py:389
  69.4 1.4 %shard_map.68 = (f32[2,512,512]{2,1,0:T(8,128)}, f32[2,512]{1,0:T(2,128)}, f32[2,2048]{1,0:T(2,128)}) custom-call(f32[2,512,512]{2,1,0:T(8,128)S(1)} %get-tuple-element.6.mu_v, f32[2,512]{1,0:T(2,128)S(1)} %get-tuple-element.7.lp_v, f32[2,2048]{1,0:T(2,128)S(1)} %get-tuple-element.8.lse_v), custom_call_target="tpu_custom_call" | custom-call | tf_op jit(solution)/shard_map/pallas_call | solution.py:433

commit v7 on v6

--- a/solution.py
+++ b/solution.py
@@ -14,7 +14,6 @@
 
 SWEEPS = 3
 HALF = 512
-HH = HALF // 2
 SHARD = 2048
 ROWS = 8192
 KC = 256
@@ -34,7 +33,7 @@
 
 def body(x_hbm, mu_hbm, lp_hbm, beta_hbm,
          mu_out, lp_out, lse_out,
-         xb, xt_ref, p_ref, rb, xpre, lp_in, beta_ref, s_ref, nacc, inv_n, mu_f, mu2, sqmu, lpb, sqx, mx_ref, lse_ref,
+         xb, xt_ref, p_ref, rb, xpre, lp_in, beta_ref, s_ref, nacc, mu_f, mu2, sqmu, lpb, sqx, mx_ref, lse_ref,
          st_own, st_rem, lpbuf, lse_snd, lse_rcv,
          loc_sem, xs, xr, ys, yr, ds, dr, own_s, own_r,
          st_s, st_r, lps, lpr, ls_s, ls_r, fxs, fxr, fds, fdr, frs, frr):
@@ -115,26 +114,24 @@
     def bc(row_vec):
         return jnp.transpose(jnp.broadcast_to(row_vec, (128, KC)))
 
-    def set_means(h, mu):
-        mu2[:, h * HH:(h + 1) * HH] = mu.astype(BF16) * jnp.asarray(-2.0, BF16)
-        sq = jnp.broadcast_to(jnp.sum(mu * mu, axis=1, keepdims=True), (KC, 128))
-        sqmu[...] = sq if h == 0 else sqmu[...] + sq
+    def set_means(mu):
+        mu2[...] = mu.astype(BF16) * jnp.asarray(-2.0, BF16)
+        sqmu[...] = jnp.broadcast_to(jnp.sum(mu * mu, axis=1, keepdims=True), (KC, 128))
 
     ld_lp.wait()
     ld_beta.wait()
     lpb[...] = bc(lp_in[pl.ds(side, 1), pl.ds(cbase, KC)])
     ld_mu.wait()
-    for h in range(2):
-        set_means(h, mu_f[:, h * HH:(h + 1) * HH])
+    set_means(mu_f[...])
 
     def prep(b):
         xt = jnp.transpose(xb[pl.ds(pl.multiple_of(b * BLK, BLK), BLK), :])
-        xt_ref[b] = xt
+        xt_ref[b // 2, :, pl.ds(pl.multiple_of(b % 2 * BLK, BLK), BLK)] = xt
         xf = xt.astype(F32)
         sqx[b] = jnp.sum(xf * xf, axis=0, keepdims=True)
 
-    def cross(b):
-        return jnp.dot(mu2[...], xt_ref[b], preferred_element_type=F32)
+    def cross(xt):
+        return jnp.dot(mu2[...], xt, preferred_element_type=F32)
 
     def soft(b, a2, beta, par):
         sq = sqx[b]
@@ -178,41 +175,36 @@
             lse_ref[:, pl.ds(pl.multiple_of((grp * GRP + j) * BLK, BLK), BLK)] = lse[j]
             rj = p_ref[grp * GRP + j] * scale[j]
             cnt = cnt + (rj[:, 0:128] + rj[:, 128:256])
-            rb[grp, :, j * BLK:(j + 1) * BLK] = rj.astype(BF16)
+            rb[grp % 2, :, j * BLK:(j + 1) * BLK] = rj.astype(BF16)
         nacc[...] = cnt
 
-    def gather(grp, h):
+    def gather(grp):
         rows = pl.ds(pl.multiple_of(grp * (GRP * BLK), GRP * BLK), GRP * BLK)
-        s_ref[h] += jnp.dot(rb[grp], xb[rows, h * HH:(h + 1) * HH], preferred_element_type=F32)
+        s_ref[...] += jnp.dot(rb[grp % 2], xb[rows, :], preferred_element_type=F32)
 
     def mstep(grp, par):
         wait_stats(grp, par)
         resp(grp, par)
-        gather(grp, 0)
-        gather(grp, 1)
+        gather(grp)
 
     def zero_sums():
         nacc[...] = jnp.zeros_like(nacc)
         s_ref[...] = jnp.zeros_like(s_ref)
 
-    def finish_counts():
+    def finish_sweep():
         n = jnp.sum(nacc[...], axis=1, keepdims=True)
         lp = jnp.log((n + PRIOR_ALPHA) / (ROWS + 4 * KC * PRIOR_ALPHA))
         lpb[...] = jnp.broadcast_to(lp, (KC, 128))
-        inv_n[...] = jnp.broadcast_to(1.0 / (n + EPS_COUNT), (KC, 128))
-
-    def finish_means(h):
-        inv = inv_n[...]
-        mu = s_ref[h] * jnp.concatenate([inv, inv], axis=1)
-        mu_out[side, pl.ds(cbase, KC), h * HH:(h + 1) * HH] = mu
-        set_means(h, mu)
+        mu = s_ref[...] * (1.0 / (n + EPS_COUNT))
+        mu_out[side, pl.ds(cbase, KC), :] = mu
+        set_means(mu)
 
     zero_sums()
     beta0 = beta_ref[0]
 
     def first_block(b):
         prep(b)
-        soft(b, cross(b), beta0, 0)
+        soft(b, cross(xt_ref[b // 2, :, pl.ds(pl.multiple_of(b % 2 * BLK, BLK), BLK)]), beta0, 0)
 
         @pl.when(b % GRP == GRP - 1)
         def _():
@@ -270,9 +262,7 @@
 
     mstep(NGRP - 2, 0)
     mstep(NGRP - 1, 0)
-    finish_counts()
-    for h in range(2):
-        finish_means(h)
+    finish_sweep()
 
     def all_sent(n, sem):
         ref = xb.at[pl.ds(0, n), :]
@@ -284,7 +274,7 @@
     all_sent(NCH * 2 * Z, ds)
 
     def block(s, q):
-        return mu_out.at[s, pl.ds(cbase + (q % 2) * (KC // 2), KC // 2), pl.ds((q // 2) * HH, HH)]
+        return mu_out.at[s, pl.ds(cbase + q * QC, QC), :]
 
     def whole(s):
         return mu_out.at[s, pl.ds(cbase, KC), :]
@@ -296,12 +286,6 @@
     def relay(q):
         ref = block(1 - side, q)
         return remote(ref, ref, frs, frr, sib)
-
-    def send_half(h):
-        for q in (2 * h, 2 * h + 1):
-            fx_copy(q).start()
-        ref = mu_out.at[side, pl.ds(cbase, KC), pl.ds(h * HH, HH)]
-        remote(ref, ref, fds, fdr, sib).start()
 
     slot = side * 2 + core
     lp_devs = (sib, xpt, xdg)
@@ -327,31 +311,22 @@
         zero_sums()
         @pl.loop(0, NBLK // 8)
         def _(i):
-            for k in range(8):
-                b = 8 * i + k
-                soft(b, cross(b), beta, par)
+            for k in range(4):
+                a2 = cross(xt_ref[4 * i + k])
+                for h in range(2):
+                    soft(8 * i + 2 * k + h, a2[:, h * BLK:(h + 1) * BLK], beta, par)
             for g in range(8 // GRP):
                 send_stats(i * (8 // GRP) + g, par)
 
         for g in range(NGRP):
-            wait_stats(g, par)
-            resp(g, par)
-            gather(g, 0)
-        finish_counts()
-        finish_means(0)
-
-        @pl.when(t == SWEEPS - 1)
-        def _():
-            send_small()
-            send_half(0)
-
-        for g in range(NGRP):
-            gather(g, 1)
-        finish_means(1)
-
-        @pl.when(t == SWEEPS - 1)
-        def _():
-            send_half(1)
+            mstep(g, par)
+        finish_sweep()
+
+    send_small()
+    for q in range(NQ):
+        fx_copy(q).start()
+    to_sib = remote(whole(side), whole(side), fds, fdr, sib)
+    to_sib.start()
 
     lse_copy.wait()
     lse_out[pl.ds(1 - side, 1), :] = lse_rcv[...]
@@ -364,7 +339,7 @@
         fx_copy(q).wait_recv()
         relay(q).start()
 
-    remote(whole(side), whole(side), fds, fdr, sib).wait()
+    to_sib.wait()
     remote(whole(1 - side), whole(1 - side), frs, frr, sib).wait()
     remote(whole(side), whole(side), fxs, frr, xpt).wait_send()
 
@@ -393,14 +368,13 @@
             out_specs=(vmem, vmem, vmem),
             scratch_shapes=[
                 pltpu.VMEM((ROWS, HALF), BF16),
-                pltpu.VMEM((NBLK, HALF, BLK), BF16),
+                pltpu.VMEM((NBLK // 2, HALF, 2 * BLK), BF16),
                 pltpu.VMEM((NBLK, KC, BLK), F32),
-                pltpu.VMEM((NGRP, KC, GRP * BLK), BF16),
+                pltpu.VMEM((2, KC, GRP * BLK), BF16),
                 pltpu.VMEM((PRE * Z, HALF), BF16),
                 pltpu.VMEM((2, 2 * KC), F32),
                 pltpu.SMEM((SWEEPS,), F32),
-                pltpu.VMEM((2, KC, HH), F32),
-                pltpu.VMEM((KC, 128), F32),
+                pltpu.VMEM((KC, HALF), F32),
                 pltpu.VMEM((KC, 128), F32),
                 pltpu.VMEM((KC, HALF), F32),
                 pltpu.VMEM((KC, HALF), BF16),

time: 70.9 us -> 68.5 us (0.966)
  Pallas kernels: 70.2 us -> 67.7 us
    pallas_call x1, Pallas kernels: 68.8 us -> 66.4 us  [local_fit(): pl.pallas_call(body, out_shape=tuple((pltpu.VMEM(o.shape, o.dtype) for o...]
where the time goes in v7:
time: 68.5 us; the launch traced here: 68.3 us
  Pallas kernels  67.7 us (99%)
    pallas_call x1, Pallas kernels, local_fit(): pl.pallas_call(body, out_shape=tuple((pltpu.VMEM(o.shape, o.dtype) for o...  66.4 us

profile of v7, /device:TPU:0, one launch (start us, length us, event | category | flops | bytes accessed | tf_op | source)
XLA Modules:
  0.0 68.3 jit_solution(4922386042949174321)
XLA Ops:
  0.6 66.4 %shard_map.67 = (f32[2,512,512]{2,1,0:T(8,128)S(1)}, f32[2,512]{1,0:T(2,128)S(1)}, f32[2,2048]{1,0:T(2,128)S(1)}) custom-call(bf16[2048,1024]{1,0:T(8,128)(2,1)} %x_hbm.1, f32[2,512,512]{2,1,0:T(8,128)} %mu_hbm.1, f32[2,512]{1,0:T(2,128)} %lp_hbm.1, f32[3]{0:T(128)} %beta_hbm.1), custom_call_target="tpu_custom_call" | custom-call | tf_op jit(solution)/shard_map/pallas_call | solution.py:364
  67.0 1.4 %shard_map.68 = (f32[2,512,512]{2,1,0:T(8,128)}, f32[2,512]{1,0:T(2,128)}, f32[2,2048]{1,0:T(2,128)}) custom-call(f32[2,512,512]{2,1,0:T(8,128)S(1)} %get-tuple-element.6.mu_v, f32[2,512]{1,0:T(2,128)S(1)} %get-tuple-element.7.lp_v, f32[2,2048]{1,0:T(2,128)S(1)} %get-tuple-element.8.lse_v), custom_call_target="tpu_custom_call" | custom-call | tf_op jit(solution)/shard_map/pallas_call | solution.py:407

commit v8 on v7

--- a/solution.py
+++ b/solution.py
@@ -148,22 +148,20 @@
             mx_ref[b, :, cols] = m
             st_own[par, grp, j, :, cols] = m + jnp.log(r)
 
-    def st_copy(grp, par, i):
-        return remote(st_own.at[par, grp], st_rem.at[par, grp, i],
-                      st_s.at[grp], st_r.at[par, grp], peers[i])
-
-    def send_stats(grp, par):
+    def send_stats(grp, par, n):
+        own = st_own.at[par, pl.ds(grp, n)]
         for i in range(3):
-            st_copy(grp, par, i).start()
-
-    def wait_stats(grp, par):
-        three = st_rem.at[par, grp]
-        both = remote(three, three, st_s.at[grp], st_r.at[par, grp], sib)
-        both.wait_recv()
-        both.wait_send()
+            remote(own, st_rem.at[par, i, pl.ds(grp, n)], st_s, st_r.at[par, grp], peers[i]).start()
+
+    def wait_stats(grp, par, n):
+        three = st_rem.at[par, :, pl.ds(grp, n)]
+        remote(three, three, st_s, st_r.at[par, grp], sib).wait_recv()
+
+    def stats_sent(par):
+        remote(st_rem.at[par], st_rem.at[par], st_s, st_r.at[par, 0], sib).wait_send()
 
     def resp(grp, par):
-        st = [st_own[par, grp]] + [st_rem[par, grp, i] for i in range(3)]
+        st = [st_own[par, grp]] + [st_rem[par, i, grp] for i in range(3)]
         top = jnp.maximum(jnp.maximum(st[0], st[1]), jnp.maximum(st[2], st[3]))
         es = [jnp.exp(v - top) for v in st]
         tot = (es[0] + es[1]) + (es[2] + es[3])
@@ -182,8 +180,9 @@
         rows = pl.ds(pl.multiple_of(grp * (GRP * BLK), GRP * BLK), GRP * BLK)
         s_ref[...] += jnp.dot(rb[grp % 2], xb[rows, :], preferred_element_type=F32)
 
-    def mstep(grp, par):
-        wait_stats(grp, par)
+    def mstep(grp, par, n=1):
+        if n:
+            wait_stats(grp, par, n)
         resp(grp, par)
         gather(grp)
 
@@ -208,7 +207,7 @@
 
         @pl.when(b % GRP == GRP - 1)
         def _():
-            send_stats(b // GRP, 0)
+            send_stats(b // GRP, 0, 1)
 
     def own_block(n):
         @pl.when((n >= 8) & (n % 2 == 0))
@@ -262,6 +261,7 @@
 
     mstep(NGRP - 2, 0)
     mstep(NGRP - 1, 0)
+    stats_sent(0)
     finish_sweep()
 
     def all_sent(n, sem):
@@ -315,11 +315,11 @@
                 a2 = cross(xt_ref[4 * i + k])
                 for h in range(2):
                     soft(8 * i + 2 * k + h, a2[:, h * BLK:(h + 1) * BLK], beta, par)
-            for g in range(8 // GRP):
-                send_stats(i * (8 // GRP) + g, par)
+            send_stats(2 * i, par, 2)
 
         for g in range(NGRP):
-            mstep(g, par)
+            mstep(g, par, 2 * (1 - g % 2))
+        stats_sent(par)
         finish_sweep()
 
     send_small()
@@ -384,7 +384,7 @@
                 pltpu.VMEM((NBLK, 1, BLK), F32),
                 pltpu.VMEM((1, ROWS), F32),
                 pltpu.VMEM((2, NGRP, GRP, 1, BLK), F32),
-                pltpu.VMEM((2, NGRP, 3, GRP, 1, BLK), F32),
+                pltpu.VMEM((2, 3, NGRP, GRP, 1, BLK), F32),
                 pltpu.VMEM((4, 1, KC), F32),
                 pltpu.VMEM((1, SHARD), F32),
                 pltpu.VMEM((1, SHARD), F32),
@@ -393,7 +393,7 @@
                 dma, dma((NCH - 1,)),
                 dma, dma((NCH,)),
                 dma, dma((NOWN,)),
-                dma((NGRP,)), dma((2, NGRP)),
+                dma, dma((2, NGRP)),
                 dma, dma,
                 dma, dma,
                 dma, dma((NQ,)),

time: 68.5 us -> 68.7 us (level)
  no operation moved by 1% of the time
where the time goes in v8:
time: 68.7 us; the launch traced here: 68.6 us
  Pallas kernels  68 us (99%)
    pallas_call x1, Pallas kernels, local_fit(): pl.pallas_call(body, out_shape=tuple((pltpu.VMEM(o.shape, o.dtype) for o...  66.7 us

profile of v8, /device:TPU:0, one launch (start us, length us, event | category | flops | bytes accessed | tf_op | source)
XLA Modules:
  0.0 68.6 jit_solution(16191592540914004359)
XLA Ops:
  0.6 66.7 %shard_map.67 = (f32[2,512,512]{2,1,0:T(8,128)S(1)}, f32[2,512]{1,0:T(2,128)S(1)}, f32[2,2048]{1,0:T(2,128)S(1)}) custom-call(bf16[2048,1024]{1,0:T(8,128)(2,1)} %x_hbm.1, f32[2,512,512]{2,1,0:T(8,128)} %mu_hbm.1, f32[2,512]{1,0:T(2,128)} %lp_hbm.1, f32[3]{0:T(128)} %beta_hbm.1), custom_call_target="tpu_custom_call" | custom-call | tf_op jit(solution)/shard_map/pallas_call | solution.py:364
  67.3 1.4 %shard_map.68 = (f32[2,512,512]{2,1,0:T(8,128)}, f32[2,512]{1,0:T(2,128)}, f32[2,2048]{1,0:T(2,128)}) custom-call(f32[2,512,512]{2,1,0:T(8,128)S(1)} %get-tuple-element.6.mu_v, f32[2,512]{1,0:T(2,128)S(1)} %get-tuple-element.7.lp_v, f32[2,2048]{1,0:T(2,128)S(1)} %get-tuple-element.8.lse_v), custom_call_target="tpu_custom_call" | custom-call | tf_op jit(solution)/shard_map/pallas_call | solution.py:407

commit v9 on v8

--- a/solution.py
+++ b/solution.py
@@ -196,7 +196,6 @@
         lpb[...] = jnp.broadcast_to(lp, (KC, 128))
         mu = s_ref[...] * (1.0 / (n + EPS_COUNT))
         mu_out[side, pl.ds(cbase, KC), :] = mu
-        set_means(mu)
 
     zero_sums()
     beta0 = beta_ref[0]
@@ -205,10 +204,6 @@
         prep(b)
         soft(b, cross(xt_ref[b // 2, :, pl.ds(pl.multiple_of(b % 2 * BLK, BLK), BLK)]), beta0, 0)
 
-        @pl.when(b % GRP == GRP - 1)
-        def _():
-            send_stats(b // GRP, 0, 1)
-
     def own_block(n):
         @pl.when((n >= 8) & (n % 2 == 0))
         def _():
@@ -255,14 +250,21 @@
             d_copy(it - 4).wait_recv()
             first_block(NBLK // 2 + it - 4)
 
-        @pl.when((it >= 9) & (it < 15))
-        def _():
-            mstep(it - 9, 0)
-
-    mstep(NGRP - 2, 0)
-    mstep(NGRP - 1, 0)
+        @pl.when(it == NCH - 2)
+        def _():
+            send_stats(0, 0, 4)
+            send_stats(4, 0, 2)
+
+        @pl.when(it == NCH - 1)
+        def _():
+            send_stats(6, 0, 1)
+
+    send_stats(7, 0, 1)
+    for g in range(NGRP):
+        mstep(g, 0, {0: 4, 4: 2, 6: 1, 7: 1}.get(g, 0))
     stats_sent(0)
     finish_sweep()
+    set_means(mu_out[side, pl.ds(cbase, KC), :])
 
     def all_sent(n, sem):
         ref = xb.at[pl.ds(0, n), :]
@@ -319,11 +321,17 @@
 
         for g in range(NGRP):
             mstep(g, par, 2 * (1 - g % 2))
+        finish_sweep()
+
+        @pl.when(t < SWEEPS - 1)
+        def _():
+            set_means(mu_out[side, pl.ds(cbase, KC), :])
+
         stats_sent(par)
-        finish_sweep()
-
+
+    fx_copy(0).start()
     send_small()
-    for q in range(NQ):
+    for q in range(1, NQ):
         fx_copy(q).start()
     to_sib = remote(whole(side), whole(side), fds, fdr, sib)
     to_sib.start()
@@ -345,7 +353,11 @@
 
 
 def write_out(mu_v, lp_v, lse_v, mu_o, lp_o, lse_o, sem):
-    pairs = ((mu_v, mu_o), (lp_v, lp_o), (lse_v, lse_o))
+    pairs = [(lp_v, lp_o), (lse_v, lse_o)]
+    for s in range(2):
+        for k in range(2):
+            part = pl.ds(k * KC, KC)
+            pairs.append((mu_v.at[s, part, :], mu_o.at[s, part, :]))
     copies = [pltpu.make_async_copy(src, dst, sem.at[i]) for i, (src, dst) in enumerate(pairs)]
     for c in copies:
         c.start()
@@ -409,7 +421,7 @@
             out_shape=tuple(outs),
             in_specs=[vmem] * 3,
             out_specs=(hbm,) * 3,
-            scratch_shapes=[dma((3,))],
+            scratch_shapes=[dma((6,))],
         )(*[pltpu.with_memory_space_constraint(r, pltpu.VMEM) for r in res])
 
     return jax.shard_map(

time: 68.7 us -> 68.4 us (level)
  no operation moved by 1% of the time
where the time goes in v9:
time: 68.4 us; the launch traced here: 68.3 us
  Pallas kernels  67.6 us (99%)
    pallas_call x1, Pallas kernels, local_fit(): pl.pallas_call(body, out_shape=tuple((pltpu.VMEM(o.shape, o.dtype) for o...  66.3 us
    pallas_call x1, Pallas kernels, local_fit(): pl.pallas_call(write_out, out_shape=tuple(outs), in_specs=[vmem] * 3, out...  1.37 us

profile of v9, /device:TPU:0, one launch (start us, length us, event | category | flops | bytes accessed | tf_op | source)
XLA Modules:
  0.0 68.3 jit_solution(16362696130310775631)
XLA Ops:
  0.6 66.3 %shard_map.67 = (f32[2,512,512]{2,1,0:T(8,128)S(1)}, f32[2,512]{1,0:T(2,128)S(1)}, f32[2,2048]{1,0:T(2,128)S(1)}) custom-call(bf16[2048,1024]{1,0:T(8,128)(2,1)} %x_hbm.1, f32[2,512,512]{2,1,0:T(8,128)} %mu_hbm.1, f32[2,512]{1,0:T(2,128)} %lp_hbm.1, f32[3]{0:T(128)} %beta_hbm.1), custom_call_target="tpu_custom_call" | custom-call | tf_op jit(solution)/shard_map/pallas_call | solution.py:376
  66.9 1.4 %shard_map.68 = (f32[2,512,512]{2,1,0:T(8,128)}, f32[2,512]{1,0:T(2,128)}, f32[2,2048]{1,0:T(2,128)}) custom-call(f32[2,512,512]{2,1,0:T(8,128)S(1)} %get-tuple-element.6.mu_v, f32[2,512]{1,0:T(2,128)S(1)} %get-tuple-element.7.lp_v, f32[2,2048]{1,0:T(2,128)S(1)} %get-tuple-element.8.lse_v), custom_call_target="tpu_custom_call" | custom-call | tf_op jit(solution)/shard_map/pallas_call | solution.py:419

commit v10 on v9

--- a/solution.py
+++ b/solution.py
@@ -224,17 +224,17 @@
             x_copy(it).wait_recv()
             y_copy(it).start()
 
-        @pl.when((it >= 3) & (it < NCH + 2))
-        def _():
-            y_copy(it - 3).wait_recv()
-            d_copy(it - 3).start()
-
         @pl.when(it == NCH + 1)
         def _():
             x_copy(NCH - 1).wait_recv()
             x_copy(NCH).wait_recv()
             d_copy(NCH - 1).start()
 
+        @pl.when((it >= 3) & (it < NCH + 2))
+        def _():
+            y_copy(it - 3).wait_recv()
+            d_copy(it - 3).start()
+
         @pl.when(it < 4)
         def _():
             @pl.loop(0, 2)
@@ -247,8 +247,9 @@
 
         @pl.when(it >= 4)
         def _():
-            d_copy(it - 4).wait_recv()
-            first_block(NBLK // 2 + it - 4)
+            g = it - 4 + (it // (NCH + 2)) * (1 - 2 * (it % 2))
+            d_copy(g).wait_recv()
+            first_block(NBLK // 2 + g)
 
         @pl.when(it == NCH - 2)
         def _():

time: 68.4 us -> 68 us (level)
  no operation moved by 1% of the time
where the time goes in v10:
time: 68 us; the launch traced here: 67.9 us
  Pallas kernels  67.3 us (99%)
    pallas_call x1, Pallas kernels, local_fit(): pl.pallas_call(body, out_shape=tuple((pltpu.VMEM(o.shape, o.dtype) for o...  65.9 us
    pallas_call x1, Pallas kernels, local_fit(): pl.pallas_call(write_out, out_shape=tuple(outs), in_specs=[vmem] * 3, out...  1.37 us

profile of v10, /device:TPU:0, one launch (start us, length us, event | category | flops | bytes accessed | tf_op | source)
XLA Modules:
  0.0 67.9 jit_solution(2116676456644002386)
XLA Ops:
  0.6 65.9 %shard_map.67 = (f32[2,512,512]{2,1,0:T(8,128)S(1)}, f32[2,512]{1,0:T(2,128)S(1)}, f32[2,2048]{1,0:T(2,128)S(1)}) custom-call(bf16[2048,1024]{1,0:T(8,128)(2,1)} %x_hbm.1, f32[2,512,512]{2,1,0:T(8,128)} %mu_hbm.1, f32[2,512]{1,0:T(2,128)} %lp_hbm.1, f32[3]{0:T(128)} %beta_hbm.1), custom_call_target="tpu_custom_call" | custom-call | tf_op jit(solution)/shard_map/pallas_call | solution.py:377
  66.5 1.4 %shard_map.68 = (f32[2,512,512]{2,1,0:T(8,128)}, f32[2,512]{1,0:T(2,128)}, f32[2,2048]{1,0:T(2,128)}) custom-call(f32[2,512,512]{2,1,0:T(8,128)S(1)} %get-tuple-element.6.mu_v, f32[2,512]{1,0:T(2,128)S(1)} %get-tuple-element.7.lp_v, f32[2,2048]{1,0:T(2,128)S(1)} %get-tuple-element.8.lse_v), custom_call_target="tpu_custom_call" | custom-call | tf_op jit(solution)/shard_map/pallas_call | solution.py:420

commit v11 on v10

--- a/solution.py
+++ b/solution.py
@@ -148,6 +148,29 @@
             mx_ref[b, :, cols] = m
             st_own[par, grp, j, :, cols] = m + jnp.log(r)
 
+    def soft_pair(b, a2, beta, par):
+        sq = jnp.concatenate([sqx[b], sqx[b + 1]], axis=1)
+        m = None
+        for c in range(0, KC, 8):
+            rows = slice(c, c + 8)
+            t = (a2[rows] + sq) + jnp.concatenate([sqmu[rows]] * 4, axis=1)
+            logit = jnp.concatenate([lpb[rows]] * 4, axis=1) - beta * t
+            p_ref[b, rows, :] = logit[:, 0:BLK]
+            p_ref[b + 1, rows, :] = logit[:, BLK:2 * BLK]
+            m = logit if m is None else jnp.maximum(m, logit)
+        m = jnp.max(m, axis=0, keepdims=True)
+        for k in range(2):
+            mk = m[:, k * BLK:(k + 1) * BLK]
+            mx_ref[b + k] = mk
+            r = None
+            for c in range(0, KC, 8):
+                rows = slice(c, c + 8)
+                e = jnp.exp(p_ref[b + k, rows, :] - mk)
+                p_ref[b + k, rows, :] = e
+                r = e if r is None else r + e
+            lse = mk + jnp.log(jnp.sum(r, axis=0, keepdims=True))
+            st_own[par, (b + k) // GRP, (b + k) % GRP] = lse
+
     def send_stats(grp, par, n):
         own = st_own.at[par, pl.ds(grp, n)]
         for i in range(3):
@@ -316,8 +339,7 @@
         def _(i):
             for k in range(4):
                 a2 = cross(xt_ref[4 * i + k])
-                for h in range(2):
-                    soft(8 * i + 2 * k + h, a2[:, h * BLK:(h + 1) * BLK], beta, par)
+                soft_pair(8 * i + 2 * k, a2, beta, par)
             send_stats(2 * i, par, 2)
 
         for g in range(NGRP):

time: 68 us -> 68 us (level)
  no operation moved by 1% of the time
where the time goes in v11:
time: 68 us; the launch traced here: 67.9 us
  Pallas kernels  67.3 us (99%)
    pallas_call x1, Pallas kernels, local_fit(): pl.pallas_call(body, out_shape=tuple((pltpu.VMEM(o.shape, o.dtype) for o...  65.9 us
    pallas_call x1, Pallas kernels, local_fit(): pl.pallas_call(write_out, out_shape=tuple(outs), in_specs=[vmem] * 3, out...  1.37 us

profile of v11, /device:TPU:0, one launch (start us, length us, event | category | flops | bytes accessed | tf_op | source)
XLA Modules:
  0.0 67.9 jit_solution(3154223078339279489)
XLA Ops:
  0.6 65.9 %shard_map.67 = (f32[2,512,512]{2,1,0:T(8,128)S(1)}, f32[2,512]{1,0:T(2,128)S(1)}, f32[2,2048]{1,0:T(2,128)S(1)}) custom-call(bf16[2048,1024]{1,0:T(8,128)(2,1)} %x_hbm.1, f32[2,512,512]{2,1,0:T(8,128)} %mu_hbm.1, f32[2,512]{1,0:T(2,128)} %lp_hbm.1, f32[3]{0:T(128)} %beta_hbm.1), custom_call_target="tpu_custom_call" | custom-call | tf_op jit(solution)/shard_map/pallas_call | solution.py:399
  66.5 1.4 %shard_map.68 = (f32[2,512,512]{2,1,0:T(8,128)}, f32[2,512]{1,0:T(2,128)}, f32[2,2048]{1,0:T(2,128)}) custom-call(f32[2,512,512]{2,1,0:T(8,128)S(1)} %get-tuple-element.6.mu_v, f32[2,512]{1,0:T(2,128)S(1)} %get-tuple-element.7.lp_v, f32[2,2048]{1,0:T(2,128)S(1)} %get-tuple-element.8.lse_v), custom_call_target="tpu_custom_call" | custom-call | tf_op jit(solution)/shard_map/pallas_call | solution.py:442

commit v12 on v10

--- a/solution.py
+++ b/solution.py
@@ -124,11 +124,12 @@
     ld_mu.wait()
     set_means(mu_f[...])
 
-    def prep(b):
-        xt = jnp.transpose(xb[pl.ds(pl.multiple_of(b * BLK, BLK), BLK), :])
-        xt_ref[b // 2, :, pl.ds(pl.multiple_of(b % 2 * BLK, BLK), BLK)] = xt
+    def prep(b, c):
+        rows = pl.ds(pl.multiple_of(b * BLK + c * 128, 128), 128)
+        xt = jnp.transpose(xb[rows, :])
+        xt_ref[b // 2, :, pl.ds(pl.multiple_of(b % 2 * BLK + c * 128, 128), 128)] = xt
         xf = xt.astype(F32)
-        sqx[b] = jnp.sum(xf * xf, axis=0, keepdims=True)
+        sqx[b, :, pl.ds(pl.multiple_of(c * 128, 128), 128)] = jnp.sum(xf * xf, axis=0, keepdims=True)
 
     def cross(xt):
         return jnp.dot(mu2[...], xt, preferred_element_type=F32)
@@ -201,7 +202,6 @@
     beta0 = beta_ref[0]
 
     def first_block(b):
-        prep(b)
         soft(b, cross(xt_ref[b // 2, :, pl.ds(pl.multiple_of(b % 2 * BLK, BLK), BLK)]), beta0, 0)
 
     def own_block(n):
@@ -209,7 +209,10 @@
         def _():
             own_copy((n - 8) // 2).wait_recv()
 
-        first_block((core * 8 + n) % 16)
+        b = (core * 8 + n) % 16
+        prep(b, 0)
+        prep(b, 1)
+        first_block(b)
 
     ld_x.wait()
 
@@ -229,11 +232,13 @@
             x_copy(NCH - 1).wait_recv()
             x_copy(NCH).wait_recv()
             d_copy(NCH - 1).start()
+            prep(NBLK - 1, core)
 
         @pl.when((it >= 3) & (it < NCH + 2))
         def _():
             y_copy(it - 3).wait_recv()
             d_copy(it - 3).start()
+            prep(NBLK // 2 + it - 3, core)
 
         @pl.when(it < 4)
         def _():
@@ -249,6 +254,7 @@
         def _():
             g = it - 4 + (it // (NCH + 2)) * (1 - 2 * (it % 2))
             d_copy(g).wait_recv()
+            prep(NBLK // 2 + g, 1 - core)
             first_block(NBLK // 2 + g)
 
         @pl.when(it == NCH - 2)
@@ -312,16 +318,23 @@
         par = t % 2
         beta = beta_ref[t]
         zero_sums()
-        @pl.loop(0, NBLK // 8)
+        def epairs(first, n):
+            for k in range(n):
+                a2 = cross(xt_ref[first + k])
+                for h in range(2):
+                    soft(2 * (first + k) + h, a2[:, h * BLK:(h + 1) * BLK], beta, par)
+
+        @pl.loop(0, NBLK // 8 - 1)
         def _(i):
-            for k in range(4):
-                a2 = cross(xt_ref[4 * i + k])
-                for h in range(2):
-                    soft(8 * i + 2 * k + h, a2[:, h * BLK:(h + 1) * BLK], beta, par)
+            epairs(4 * i, 4)
             send_stats(2 * i, par, 2)
 
+        for g in (NGRP - 2, NGRP - 1):
+            epairs(2 * g, 2)
+            send_stats(g, par, 1)
+
         for g in range(NGRP):
-            mstep(g, par, 2 * (1 - g % 2))
+            mstep(g, par, 1 if g >= NGRP - 2 else 2 * (1 - g % 2))
         finish_sweep()
 
         @pl.when(t < SWEEPS - 1)

time: 68 us -> 67.8 us (level)
  no operation moved by 1% of the time
where the time goes in v12:
time: 67.8 us; the launch traced here: 67.7 us
  Pallas kernels  67.1 us (99%)
    pallas_call x1, Pallas kernels, local_fit(): pl.pallas_call(body, out_shape=tuple((pltpu.VMEM(o.shape, o.dtype) for o...  65.7 us
    pallas_call x1, Pallas kernels, local_fit(): pl.pallas_call(write_out, out_shape=tuple(outs), in_specs=[vmem] * 3, out...  1.37 us

profile of v12, /device:TPU:0, one launch (start us, length us, event | category | flops | bytes accessed | tf_op | source)
XLA Modules:
  0.0 67.7 jit_solution(385329475392455017)
XLA Ops:
  0.6 65.7 %shard_map.67 = (f32[2,512,512]{2,1,0:T(8,128)S(1)}, f32[2,512]{1,0:T(2,128)S(1)}, f32[2,2048]{1,0:T(2,128)S(1)}) custom-call(bf16[2048,1024]{1,0:T(8,128)(2,1)} %x_hbm.1, f32[2,512,512]{2,1,0:T(8,128)} %mu_hbm.1, f32[2,512]{1,0:T(2,128)} %lp_hbm.1, f32[3]{0:T(128)} %beta_hbm.1), custom_call_target="tpu_custom_call" | custom-call | tf_op jit(solution)/shard_map/pallas_call | solution.py:390
  66.4 1.4 %shard_map.68 = (f32[2,512,512]{2,1,0:T(8,128)}, f32[2,512]{1,0:T(2,128)}, f32[2,2048]{1,0:T(2,128)}) custom-call(f32[2,512,512]{2,1,0:T(8,128)S(1)} %get-tuple-element.6.mu_v, f32[2,512]{1,0:T(2,128)S(1)} %get-tuple-element.7.lp_v, f32[2,2048]{1,0:T(2,128)S(1)} %get-tuple-element.8.lse_v), custom_call_target="tpu_custom_call" | custom-call | tf_op jit(solution)/shard_map/pallas_call | solution.py:433

commit v13 on v12

--- a/solution.py
+++ b/solution.py
@@ -220,7 +220,7 @@
     def _(n):
         own_block(n)
 
-    @pl.loop(0, NCH + 4)
+    @pl.loop(0, NCH + 2)
     def _(it):
         @pl.when(it < NCH - 1)
         def _():
@@ -252,10 +252,9 @@
 
         @pl.when(it >= 4)
         def _():
-            g = it - 4 + (it // (NCH + 2)) * (1 - 2 * (it % 2))
-            d_copy(g).wait_recv()
-            prep(NBLK // 2 + g, 1 - core)
-            first_block(NBLK // 2 + g)
+            d_copy(it - 4).wait_recv()
+            prep(NBLK // 2 + it - 4, 1 - core)
+            first_block(NBLK // 2 + it - 4)
 
         @pl.when(it == NCH - 2)
         def _():
@@ -266,6 +265,12 @@
         def _():
             send_stats(6, 0, 1)
 
+    for g in (NCH - 1, NCH - 2):
+        d_copy(g).wait_recv()
+        prep(NBLK // 2 + g, 1 - core)
+    a2 = cross(xt_ref[NBLK // 2 - 1])
+    for h in range(2):
+        soft(NBLK - 2 + h, a2[:, h * BLK:(h + 1) * BLK], beta0, 0)
     send_stats(7, 0, 1)
     for g in range(NGRP):
         mstep(g, 0, {0: 4, 4: 2, 6: 1, 7: 1}.get(g, 0))

time: 67.8 us -> 67.8 us (level)
  no operation moved by 1% of the time
where the time goes in v13:
time: 67.8 us; the launch traced here: 67.6 us
  Pallas kernels  67 us (99%)
    pallas_call x1, Pallas kernels, local_fit(): pl.pallas_call(body, out_shape=tuple((pltpu.VMEM(o.shape, o.dtype) for o...  65.6 us
    pallas_call x1, Pallas kernels, local_fit(): pl.pallas_call(write_out, out_shape=tuple(outs), in_specs=[vmem] * 3, out...  1.37 us

profile of v13, /device:TPU:0, one launch (start us, length us, event | category | flops | bytes accessed | tf_op | source)
XLA Modules:
  0.0 67.6 jit_solution(7869563183118971586)
XLA Ops:
  0.6 65.6 %shard_map.67 = (f32[2,512,512]{2,1,0:T(8,128)S(1)}, f32[2,512]{1,0:T(2,128)S(1)}, f32[2,2048]{1,0:T(2,128)S(1)}) custom-call(bf16[2048,1024]{1,0:T(8,128)(2,1)} %x_hbm.1, f32[2,512,512]{2,1,0:T(8,128)} %mu_hbm.1, f32[2,512]{1,0:T(2,128)} %lp_hbm.1, f32[3]{0:T(128)} %beta_hbm.1), custom_call_target="tpu_custom_call" | custom-call | tf_op jit(solution)/shard_map/pallas_call | solution.py:395
  66.3 1.4 %shard_map.68 = (f32[2,512,512]{2,1,0:T(8,128)}, f32[2,512]{1,0:T(2,128)}, f32[2,2048]{1,0:T(2,128)}) custom-call(f32[2,512,512]{2,1,0:T(8,128)S(1)} %get-tuple-element.6.mu_v, f32[2,512]{1,0:T(2,128)S(1)} %get-tuple-element.7.lp_v, f32[2,2048]{1,0:T(2,128)S(1)} %get-tuple-element.8.lse_v), custom_call_target="tpu_custom_call" | custom-call | tf_op jit(solution)/shard_map/pallas_call | solution.py:438

commit v14 on v13

--- a/solution.py
+++ b/solution.py
@@ -27,8 +27,8 @@
 NOWN = 4
 PIECE = SHARD // NOWN
 OWN = 2 * SHARD
-NQ = 4
-QC = KC // NQ
+NQ = 5
+QUARTERS = ((0, 64), (64, 64), (128, 64), (192, 48), (240, 16))
 
 
 def body(x_hbm, mu_hbm, lp_hbm, beta_hbm,
@@ -288,7 +288,7 @@
     all_sent(NCH * 2 * Z, ds)
 
     def block(s, q):
-        return mu_out.at[s, pl.ds(cbase + q * QC, QC), :]
+        return mu_out.at[s, pl.ds(cbase + QUARTERS[q][0], QUARTERS[q][1]), :]
 
     def whole(s):
         return mu_out.at[s, pl.ds(cbase, KC), :]

time: 67.8 us -> 67.6 us (level)
  no operation moved by 1% of the time
where the time goes in v14:
time: 67.6 us; the launch traced here: 67.5 us
  Pallas kernels  66.9 us (99%)
    pallas_call x1, Pallas kernels, local_fit(): pl.pallas_call(body, out_shape=tuple((pltpu.VMEM(o.shape, o.dtype) for o...  65.5 us
    pallas_call x1, Pallas kernels, local_fit(): pl.pallas_call(write_out, out_shape=tuple(outs), in_specs=[vmem] * 3, out...  1.37 us

profile of v14, /device:TPU:0, one launch (start us, length us, event | category | flops | bytes accessed | tf_op | source)
XLA Modules:
  0.0 67.5 jit_solution(15387909603722953419)
XLA Ops:
  0.6 65.5 %shard_map.67 = (f32[2,512,512]{2,1,0:T(8,128)S(1)}, f32[2,512]{1,0:T(2,128)S(1)}, f32[2,2048]{1,0:T(2,128)S(1)}) custom-call(bf16[2048,1024]{1,0:T(8,128)(2,1)} %x_hbm.1, f32[2,512,512]{2,1,0:T(8,128)} %mu_hbm.1, f32[2,512]{1,0:T(2,128)} %lp_hbm.1, f32[3]{0:T(128)} %beta_hbm.1), custom_call_target="tpu_custom_call" | custom-call | tf_op jit(solution)/shard_map/pallas_call | solution.py:395
  66.1 1.4 %shard_map.68 = (f32[2,512,512]{2,1,0:T(8,128)}, f32[2,512]{1,0:T(2,128)}, f32[2,2048]{1,0:T(2,128)}) custom-call(f32[2,512,512]{2,1,0:T(8,128)S(1)} %get-tuple-element.6.mu_v, f32[2,512]{1,0:T(2,128)S(1)} %get-tuple-element.7.lp_v, f32[2,2048]{1,0:T(2,128)S(1)} %get-tuple-element.8.lse_v), custom_call_target="tpu_custom_call" | custom-call | tf_op jit(solution)/shard_map/pallas_call | solution.py:438
